TPU v7x, 32 devices: a whole 2x2x4 slice. The times are simulated.
32 devices in a mesh: row: 8 (over z, x), col: 2 (over core), dp: 2 (over y).
Axes of the slice: x: 2, y: 2, z: 4, core: 2. Of those that a mesh axis runs over, the one named last changes fastest.
Arguments:
- pixels: bfloat16 [2, 3, 256, 256], P('dp', None, 'row', 'col'), may hold values from -6 to 6
- cotangent: bfloat16 [2, 64, 64, 1024], P('dp', 'row', 'col'), may hold values from -6 to 6
- embed_weight: bfloat16 [48, 1024], replicated, may hold values from -0.875 to 0.875
- embed_bias: float32 [1024], replicated, may hold values from -4 to 4
- layer_norm_gain: float32 [1024], replicated, may hold values from 0.5 to 1.5
- qkv_weight: bfloat16 [1024, 2304], P('row', ('col', 'dp')), may hold values from -0.1875 to 0.1875
- out_weight: bfloat16 [768, 1024], P('row', ('col', 'dp')), may hold values from -0.21875 to 0.21875
- bias_table: float32 [12, 225], replicated, may hold values from -4 to 404
- rel_index: int32 [64, 64], replicated, may hold values from 0 to 224
- shifts: int32 [2, 2], P('dp'), may hold values from 1 to 7
Outputs:
- out_weight_grad: float32 [768, 1024], P('row', ('col', 'dp'))
- embed_weight_grad: float32 [48, 1024], replicated
- embed_bias_grad: float32 [1024], replicated
- norm_gain_grad: float32 [1024], replicated
- bias_table_grad: float32 [12, 225], replicated
Inputs may be any that keep to these rules, and one draw needn't show every extreme that they name: `rel_index`: each entry names one of the 225 columns of bias_table.
All inputs are finite; a program needn't handle non-finite values.
Results may differ from a plain program's by a relative error of at most 0.023.
Values may be sent and summed in bfloat16 or wider, within the bound.
A program may use at most 64 MiB of HBM per device.

v0:
```python
import jax
import jax.numpy as jnp
from jax import lax
from jax.sharding import PartitionSpec as P

WIN = 8
PATCH = 4


norm_epsilon = 1e-05


def from_behind(value, axis, steps):
    count = lax.axis_size(axis)
    pairs = [(source, (source + steps) % count) for source in range(count)]
    return lax.ppermute(value, axis, pairs)


def make_patches(pixel_block):
    images, channels, pixel_rows, pixel_cols = pixel_block.shape
    grid_rows = pixel_rows // PATCH
    grid_cols = pixel_cols // PATCH
    shaped = pixel_block.reshape(images, channels, grid_rows, PATCH, grid_cols, PATCH)
    return shaped.transpose(0, 2, 4, 1, 3, 5).reshape(
        images, grid_rows, grid_cols, channels * PATCH * PATCH
    )


def embed_cells(patches, embed_weight, embed_bias):
    return (jnp.dot(patches, embed_weight, preferred_element_type=jnp.float32) + embed_bias).astype(
        jnp.bfloat16
    )


def window_split(block):
    rows_all, cols_all, features = block.shape
    shaped = block.reshape(rows_all // WIN, WIN, cols_all // WIN, WIN, features)
    return shaped.transpose(0, 2, 1, 3, 4).reshape(-1, WIN * WIN, features)


def window_join(windows, rows_all, cols_all):
    features = windows.shape[-1]
    shaped = windows.reshape(rows_all // WIN, cols_all // WIN, WIN, WIN, features)
    return shaped.transpose(0, 2, 1, 3, 4).reshape(rows_all, cols_all, features)


def splice_after(own_block, borrowed, offsets, along_dim):
    length = own_block.shape[along_dim]

    def single(own_item, borrowed_item, offset):
        joined = jnp.concatenate([own_item, borrowed_item], along_dim - 1)
        return lax.dynamic_slice_in_dim(joined, offset, length, along_dim - 1)

    return jax.vmap(single)(own_block, borrowed, offsets)


def splice_before(own_block, borrowed, offsets, along_dim):
    length = own_block.shape[along_dim]
    margin = borrowed.shape[along_dim]

    def single(own_item, borrowed_item, offset):
        joined = jnp.concatenate([borrowed_item, own_item], along_dim - 1)
        return lax.dynamic_slice_in_dim(joined, margin - offset, length, along_dim - 1)

    return jax.vmap(single)(own_block, borrowed, offsets)


def attend_forward(cell_windows, labels, layer_norm_gain, qkv_full, bias_full):
    window_count, cell_count, features = cell_windows.shape
    head_count = bias_full.shape[0]
    inner_width = qkv_full.shape[1] // 3
    head_size = inner_width // head_count
    score_scale = head_size ** (-0.5)
    flat_rows = cell_windows.reshape(-1, features).astype(jnp.float32)
    average = jnp.mean(flat_rows, axis=-1, keepdims=True)
    centered_input = flat_rows - average
    inverse_deviation = lax.rsqrt(
        jnp.mean(centered_input * centered_input, axis=-1, keepdims=True) + norm_epsilon
    )
    standardized_rows = centered_input * inverse_deviation
    normalized_rows = (standardized_rows * layer_norm_gain).astype(jnp.bfloat16)
    projected = jnp.dot(normalized_rows, qkv_full, preferred_element_type=jnp.float32).astype(
        jnp.bfloat16
    )
    head_shape = (window_count, cell_count, head_count, head_size)
    query_rows = projected[:, :inner_width].reshape(head_shape)
    key_vectors = projected[:, inner_width : 2 * inner_width].reshape(head_shape)
    value_rows = projected[:, 2 * inner_width :].reshape(head_shape)
    scores = (
        jnp.einsum("wmhd,wnhd->whmn", query_rows, key_vectors, preferred_element_type=jnp.float32)
        * score_scale
        + bias_full[None]
    )
    same_region = labels[:, None, :, None] == labels[:, None, None, :]
    scores = jnp.where(same_region, scores, -1e30)
    row_peak = jnp.max(scores, axis=-1, keepdims=True)
    exp_scores = jnp.exp(scores - row_peak)
    attention_weights = exp_scores / jnp.sum(exp_scores, axis=-1, keepdims=True)
    reduced_probability = attention_weights.astype(jnp.bfloat16)
    attended = jnp.einsum(
        "whmn,wnhd->wmhd", reduced_probability, value_rows, preferred_element_type=jnp.float32
    ).astype(jnp.bfloat16)
    stored_residuals = (
        standardized_rows,
        inverse_deviation,
        query_rows,
        key_vectors,
        value_rows,
        attention_weights,
        reduced_probability,
    )
    return (stored_residuals, attended.reshape(-1, inner_width))


def attend_backward(stored_residuals, d_attended, layer_norm_gain, qkv_full):
    (
        standardized_rows,
        inverse_deviation,
        query_rows,
        key_vectors,
        value_rows,
        attention_weights,
        reduced_probability,
    ) = stored_residuals
    head_shape = query_rows.shape
    score_scale = head_shape[3] ** (-0.5)
    total_row_count = standardized_rows.shape[0]
    inner_width = head_shape[2] * head_shape[3]
    d_heads = d_attended.reshape(head_shape)
    d_prob = jnp.einsum("wmhd,wnhd->whmn", d_heads, value_rows, preferred_element_type=jnp.float32)
    d_values = jnp.einsum(
        "whmn,wmhd->wnhd", reduced_probability, d_heads, preferred_element_type=jnp.float32
    ).astype(jnp.bfloat16)
    d_scores = attention_weights * (
        d_prob - jnp.sum(attention_weights * d_prob, axis=-1, keepdims=True)
    )
    table_part = jnp.sum(d_scores, axis=0)
    d_low = d_scores.astype(jnp.bfloat16)
    d_queries = (
        jnp.einsum("whmn,wnhd->wmhd", d_low, key_vectors, preferred_element_type=jnp.float32)
        * score_scale
    ).astype(jnp.bfloat16)
    d_keys = (
        jnp.einsum("whmn,wmhd->wnhd", d_low, query_rows, preferred_element_type=jnp.float32)
        * score_scale
    ).astype(jnp.bfloat16)
    d_projected = jnp.concatenate(
        [
            d_queries.reshape(total_row_count, inner_width),
            d_keys.reshape(total_row_count, inner_width),
            d_values.reshape(total_row_count, inner_width),
        ],
        axis=1,
    )
    normalized_gradient = lax.dot_general(
        d_projected, qkv_full, (((1,), (1,)), ((), ())), preferred_element_type=jnp.float32
    )
    gain_contribution = jnp.sum(normalized_gradient * standardized_rows, axis=0)
    scaled_rows = normalized_gradient * layer_norm_gain
    branch_gradient = inverse_deviation * (
        scaled_rows
        - jnp.mean(scaled_rows, axis=-1, keepdims=True)
        - standardized_rows * jnp.mean(scaled_rows * standardized_rows, axis=-1, keepdims=True)
    )
    return (branch_gradient.astype(jnp.bfloat16), gain_contribution, table_part)


def on_device(
    pixels,
    cotangent,
    embed_weight,
    embed_bias,
    layer_norm_gain,
    qkv_weight,
    out_weight,
    bias_table,
    rel_index,
    shifts,
):
    images, rows_dev, cols_dev, features = cotangent.shape
    head_count = bias_table.shape[0]
    grid_rows = rows_dev * lax.axis_size("row")
    grid_cols = cols_dev * lax.axis_size("col")
    row_shift = shifts[:, 0]
    col_shift = shifts[:, 1]
    qkv_rowwise = lax.all_gather(qkv_weight, "row", axis=0, tiled=True)
    qkv_full, out_columns = (
        lax.all_gather(qkv_rowwise, ("col", "dp"), axis=1, tiled=True),
        lax.all_gather(out_weight, ("col", "dp"), axis=1, tiled=True),
    )
    patches = make_patches(pixels)
    tokens = embed_cells(patches, embed_weight, embed_bias)
    below = from_behind((tokens, cotangent), "row", -1)
    shifted = splice_after(tokens, below[0], row_shift, 1)
    shifted_cot = splice_after(cotangent, below[1], row_shift, 1)
    beside = from_behind((shifted[:, :, :WIN], shifted_cot[:, :, :WIN]), "col", -1)
    shifted = splice_after(shifted, beside[0], col_shift, 2)
    shifted_cot = splice_after(shifted_cot, beside[1], col_shift, 2)
    row_ids = lax.axis_index("row") * rows_dev + jnp.arange(rows_dev, dtype=jnp.int32)
    col_ids = lax.axis_index("col") * cols_dev + jnp.arange(cols_dev, dtype=jnp.int32)
    row_part = (row_ids[None, :] >= grid_rows - row_shift[:, None]).astype(jnp.int32)
    col_part = (col_ids[None, :] >= grid_cols - col_shift[:, None]).astype(jnp.int32)
    region = 2 * row_part[:, :, None] + col_part[:, None, :]
    labels = window_split(region.reshape(images * rows_dev, cols_dev, 1))[:, :, 0]
    cell_windows = window_split(shifted.reshape(images * rows_dev, cols_dev, features))
    cot_flat = window_split(shifted_cot.reshape(images * rows_dev, cols_dev, features)).reshape(
        -1, features
    )
    selector = (
        rel_index.reshape(-1)[:, None] == jnp.arange(bias_table.shape[1], dtype=jnp.int32)[None, :]
    ).astype(jnp.float32)
    bias_full = jnp.dot(selector, bias_table.T, precision=lax.Precision.HIGHEST).T.reshape(
        head_count, WIN * WIN, WIN * WIN
    )
    stored_residuals, attended = attend_forward(
        cell_windows, labels, layer_norm_gain, qkv_full, bias_full
    )
    d_attended = lax.dot_general(
        cot_flat,
        lax.all_gather(out_columns, "row", axis=0, tiled=True),
        (((1,), (1,)), ((), ())),
        preferred_element_type=jnp.float32,
    ).astype(jnp.bfloat16)
    partial_rows = lax.psum_scatter(
        lax.dot_general(
            attended, cot_flat, (((0,), (0,)), ((), ())), preferred_element_type=jnp.float32
        ),
        "row",
        scatter_dimension=0,
        tiled=True,
    )
    out_weight_grad = lax.psum_scatter(partial_rows, ("col", "dp"), scatter_dimension=1, tiled=True)
    d_rows, gain_contribution, table_part = attend_backward(
        stored_residuals, d_attended, layer_norm_gain, qkv_full
    )
    branch_gradient = window_join(
        d_rows.reshape(-1, WIN * WIN, features), images * rows_dev, cols_dev
    ).reshape(images, rows_dev, cols_dev, features)
    patch_rows = patches.reshape(-1, patches.shape[-1])
    cot_rows = cotangent.reshape(-1, features)
    contract = (((0,), (0,)), ((), ()))
    behind = from_behind(branch_gradient[:, :, cols_dev - WIN :], "col", 1)
    d_back = splice_before(branch_gradient, behind, col_shift, 2)
    above = from_behind(d_back, "row", 1)
    d_back = splice_before(d_back, above, row_shift, 1)
    back_rows = d_back.reshape(-1, features)
    embed_grad = lax.dot_general(
        patch_rows, cot_rows, contract, preferred_element_type=jnp.float32
    ) + lax.dot_general(patch_rows, back_rows, contract, preferred_element_type=jnp.float32)
    bias_grad = jnp.sum(cot_rows, axis=0, dtype=jnp.float32) + jnp.sum(
        back_rows, axis=0, dtype=jnp.float32
    )
    table_grad = jnp.dot(
        table_part.reshape(head_count, -1), selector, precision=lax.Precision.HIGHEST
    )
    totals = lax.psum((embed_grad, bias_grad, gain_contribution, table_grad), ("row", "col", "dp"))
    return (out_weight_grad, totals[0], totals[1], totals[2], totals[3])


def solution(mesh):
    return jax.shard_map(
        on_device,
        mesh=mesh,
        in_specs=(
            P("dp", None, "row", "col"),
            P("dp", "row", "col", None),
            P(),
            P(),
            P(),
            P("row", ("col", "dp")),
            P("row", ("col", "dp")),
            P(),
            P(),
            P("dp", None),
        ),
        out_specs=(P("row", ("col", "dp")), P(), P(), P(), P()),
        check_vma=False,
    )
```

profile of v0, /device:TPU:0, one launch (start us, length us, event | category | flops | bytes accessed | tf_op | source)
XLA Modules:
  0.0 390.5 jit_solution(13253919688802146951)
XLA Ops:
  7.2 0.7 all-gather.4.cloned.1.call-update
  8.0 45.2 %all-gather.4.cloned.1.call-done = bf16[1024,576]{0,1:T(8,128)(2,1)} async-done(((bf16[128,576]{0,1:T(8,128)(2,1)}), bf16[1024,576]{0,1:T(8,128)(2,1)}) %all-gather.4.cloned.1.call-update) | async-done | bytes 1179664 | tf_op jit(solution)/shard_map/all_gather | solution.py:186
  53.2 2.1 collective-permute-start.2
  55.4 2.4 reshape.177
  57.8 0.7 copy.154
  58.5 0.3 fusion.11
  58.8 1.2 collective-permute-start
  60.0 12.5 %all_gather.14 = bf16[96,1024]{1,0:T(8,128)(2,1)} all-gather(bf16[96,256]{1,0:T(8,128)(2,1)S(1)} %copy-done.13), channel_id=1, replica_groups=mesh['row'=8,'col'=2,'dp'=2] {'col','dp'}, dimensions={1}, use_global_device_ids=true | all-gather | bytes 245760 | tf_op jit(solution)/shard_map/all_gather | solution.py:189
  72.6 0.6 fusion.44
  76.8 2.6 convolution_bitcast_fusion
  79.4 0.2 fusion.32
  81.3 0.9 copy.165
  82.9 0.2 fusion.31
  83.1 0.6 collective-permute-start.3
  83.7 0.4 fusion.42
  84.2 0.5 collective-permute-done.3
  84.6 0.3 fusion.27
  84.9 0.8 copy.169
  85.9 0.3 multiply_reduce_fusion.3
  86.2 0.2 copy-done.15
  86.5 0.2 multiply_convert_fusion.3
  86.7 7.0 %all-gather.6.cloned.1.call-done = bf16[1024,2304]{0,1:T(8,128)(2,1)} async-done(((bf16[1024,576]{0,1:T(8,128)(2,1)}), bf16[1024,2304]{0,1:T(8,128)(2,1)}) %all-gather.6.cloned.1.call-update) | async-done | bytes 4718608 | tf_op jit(solution)/shard_map/all_gather | solution.py:188
  93.7 3.8 convolution_convert_fusion
  97.5 1.0 fusion.43
  98.4 0.6 reshape.368
  99.1 0.9 copy.174
  99.9 2.5 reshape.366
  102.5 1.6 reshape.367
  104.1 1.8 copy.178
  105.9 1.4 add_select_fusion
  107.3 1.6 fusion.45
  109.0 3.8 fusion.7
  112.7 2.7 copy.168
  115.4 2.5 reshape.182
  117.9 3.4 fusion.46
  121.3 0.2 all-reduce.5.cloned.1.call-start
  121.5 17.9 %all-gather.8.cloned.1.call-done = bf16[768,1024]{1,0:T(8,128)(2,1)} async-done(((bf16[96,1024]{1,0:T(8,128)(2,1)}), bf16[768,1024]{1,0:T(8,128)(2,1)}) %all-gather.8.cloned.1.call-update) | async-done | bytes 1572880 | tf_op jit(solution)/shard_map/all_gather | solution.py:220
  139.4 3.0 convolution_convert_fusion.3
  142.4 2.4 reshape.369
  144.8 2.5 copy.182
  147.3 2.8 multiply_reduce_fusion
  150.1 1.3 fusion.20
  151.4 0.9 copy-done.1
  152.3 1.5 fusion.9
  153.8 2.3 copy.177
  156.0 2.5 reshape.185
  158.5 1.4 fusion.10
  160.0 1.6 copy.181
  161.6 1.2 reshape.186
  162.8 3.5 fusion.8
  166.3 1.8 copy.184
  168.1 1.2 reshape.187
  169.3 4.2 %multiply_reduce_fusion.1 = (f32[1024]{0:T(1024)S(1)}, f32[256]{0:T(256)S(1)}, f32[256]{0:T(256)S(1)}, f32[256,1024]{1,0:T(8,128)S(1)}) fusion(f32[1,4,8,8,1024]{4,3,2,1,0:T(8,128)S(1)} %copy.156, f32[256]{0:T(256)S(1)} %rsqrt.12, f32[256]{0:T(256)S(1)} %div.23, f32[1024]{0:T(1024)S(1)} %copy-done.15, bf16[1024,2304]{0,1:T(8,128)(2,1)} %all-gather.6.cloned.1.call-done, ...), kind=kOutput, calls=%fused_computation.41 | convolution fusion | flops 1213594112 | bytes 8007680 | tf_op jit(solution)/shard_map/dot_general | solution.py:155
  173.5 0.3 multiply_convert_fusion.2
  175.6 0.4 collective-permute-start.5
  177.6 15.2 %collective-permute-done.5 = bf16[1,8,32,1024]{3,2,1,0:T(8,128)(2,1)S(1)} collective-permute-done((bf16[1,8,32,1024]{3,2,1,0:T(8,128)(2,1)S(1)}, bf16[1,8,32,1024]{3,2,1,0:T(8,128)(2,1)S(1)}, u32[]{:S(2)}, u32[]{:S(2)}) %collective-permute-start.5) | collective-permute-done | bytes 524320 | tf_op jit(solution)/shard_map/ppermute | solution.py:16
  192.7 0.3 convert_reduce_fusion
  193.0 0.9 fusion.18
  194.0 33.6 %reduce-scatter.3.cloned.1.call-done = f32[96,1024]{1,0:T(8,128)} async-done(((f32[768,1024]{1,0:T(8,128)}), f32[96,1024]{1,0:T(8,128)}) %reduce-scatter.3.cloned.1.call-update) | async-done | bytes 393232 | tf_op jit(solution)/shard_map/reduce_scatter | solution.py:224
  228.1 1.4 fusion.1
  229.5 40.2 %all-reduce.2 = (f32[1024]{0:T(1024)}, f32[1024]{0:T(1024)}, f32[12,225]{1,0:T(8,128)}) all-reduce(f32[1024]{0:T(1024)S(1)} %add.134, f32[1024]{0:T(1024)S(1)} %get-tuple-element.71, f32[12,225]{1,0:T(8,128)S(1)} %fusion.1), channel_id=1, replica_groups=mesh['row'=8,'col'=2,'dp'=2] {'row','col','dp'}, use_global_device_ids=true, to_apply=%region_12.13 | all-reduce | flops 4748 | bytes 37984 | tf_op jit(solution)/shard_map/psum | solution.py:256
  269.7 87.6 %all-reduce.5.cloned.1.call-done = f32[48,1024]{1,0:T(8,128)} async-done(((f32[48,1024]{1,0:T(8,128)}), f32[48,1024]{1,0:T(8,128)}) %all-reduce.5.cloned.1.call-update) | async-done | bytes 196624 | tf_op jit(solution)/shard_map/psum | solution.py:256
  357.4 24.7 %reduce-scatter.5.cloned.1.call-done = f32[96,256]{1,0:T(8,128)} async-done(((f32[96,1024]{1,0:T(8,128)}), f32[96,256]{1,0:T(8,128)}) %reduce-scatter.5.cloned.1.call-update) | async-done | bytes 98320 | tf_op jit(solution)/shard_map/reduce_scatter | solution.py:232
  382.1 1.6 copy.218
  (81 shorter events, 2.4 us)
Async XLA Ops:
  7.2 51.3 %copy-start = (bf16[48,1024]{1,0:T(8,128)(2,1)S(1)}, bf16[48,1024]{1,0:T(8,128)(2,1)}, u32[]{:S(2)}) copy-start(bf16[48,1024]{1,0:T(8,128)(2,1)} %param.12) | copy-start | bytes 294916
  7.2 51.3 %copy-start.18 = (f32[1024]{0:T(1024)S(1)}, f32[1024]{0:T(1024)}, u32[]{:S(2)}) copy-start(f32[1024]{0:T(1024)} %param.13) | copy-start | bytes 12292
  7.2 45.9 %all-gather.4.cloned.1.call-start = ((), (), s32[]{:S(2)}) async-start(), calls=%async_computation.2 | async-start | bytes 1327104 | tf_op jit(solution)/shard_map/all_gather | solution.py:186
  7.9 85.8 %all-gather.6.cloned.1.call-start = ((), (), s32[]{:S(2)}) async-start(), calls=%async_computation.3 | async-start | bytes 5898240 | tf_op jit(solution)/shard_map/all_gather | solution.py:188
  53.1 6.9 %copy-start.13 = (bf16[96,256]{1,0:T(8,128)(2,1)S(1)}, bf16[96,256]{1,0:T(8,128)(2,1)}, u32[]{:S(2)}) copy-start(bf16[96,256]{1,0:T(8,128)(2,1)} %param.16) | copy-start | bytes 147460
  53.2 19.5 %copy-start.19 = (s32[1,2]{1,0:T(1,128)S(1)}, s32[1,2]{1,0:T(1,128)}, u32[]{:S(2)}) copy-start(s32[1,2]{1,0:T(1,128)} %param.19) | copy-start | bytes 28
  53.2 22.8 %copy-start.14 = (s32[64,64]{1,0:T(8,128)S(1)}, s32[64,64]{1,0:T(8,128)}, u32[]{:S(2)}) copy-start(s32[64,64]{1,0:T(8,128)} %param.18) | copy-start | bytes 49156
  53.2 23.6 %copy-start.20 = (f32[12,225]{1,0:T(8,128)S(1)}, f32[12,225]{1,0:T(8,128)}, u32[]{:S(2)}) copy-start(f32[12,225]{1,0:T(8,128)} %param.17) | copy-start | bytes 32404
  53.2 86.2 %all-gather.8.cloned.1.call-start = ((), (), s32[]{:S(2)}) async-start(), calls=%async_computation.6 | async-start | bytes 1769472 | tf_op jit(solution)/shard_map/all_gather | solution.py:220
  53.2 29.6 %collective-permute-start.2 = (bf16[1,8,32,1024]{3,2,1,0:T(8,128)(2,1)}, bf16[1,8,32,1024]{3,2,1,0:T(8,128)(2,1)S(1)}, u32[]{:S(2)}, u32[]{:S(2)}) collective-permute-start(bf16[1,8,32,1024]{3,2,1,0:T(8,128)(2,1)} %param.11), channel_id=1, source_target_pairs={{0,28},{4,0},{8,4},{12,8},{16,12},{20,16},{24,20},{28,24},{1,29},{... | collective-permute-start | bytes 1572872 | tf_op jit(solution)/shard_map/ppermute | solution.py:16
  58.5 20.9 %copy-start.8 = (bf16[1,8,32,3,4,4]{2,1,5,4,3,0:T(8,128)(2,1)}, bf16[1,8,32,3,4,4]{2,1,5,4,3,0:T(8,128)(2,1)S(1)}, u32[]{:S(2)}) copy-start(bf16[1,8,32,3,4,4]{2,1,5,4,3,0:T(8,128)(2,1)S(1)} %copy.154) | copy-start | bytes 73732
  58.8 20.5 %collective-permute-start = (bf16[1,8,32,1024]{3,2,1,0:T(8,128)(2,1)S(1)}, bf16[1,8,32,1024]{3,2,1,0:T(8,128)(2,1)S(1)}, u32[]{:S(2)}, u32[]{:S(2)}) collective-permute-start(bf16[1,8,32,1024]{3,2,1,0:T(8,128)(2,1)S(1)} %fusion.11), channel_id=1, source_target_pairs={{0,28},{4,0},{8,4},{12,8},{16,12},{20,16},{24,20},{28,24},{1,29},{... | collective-permute-start | bytes 1572872 | tf_op jit(solution)/shard_map/ppermute | solution.py:16
  72.6 155.0 %reduce-scatter.3.cloned.1.call-start = ((), (), s32[]{:S(2)}) async-start(), calls=%async_computation.4 | async-start | bytes 3538944 | tf_op jit(solution)/shard_map/reduce_scatter | solution.py:224
  76.1 3.3 copy-start.16
  79.4 3.5 copy-start.5
  79.6 4.0 %collective-permute-start.1 = (bf16[1,8,8,1024]{3,2,1,0:T(8,128)(2,1)S(1)}, bf16[1,8,8,1024]{3,2,1,0:T(8,128)(2,1)S(1)}, u32[]{:S(2)}, u32[]{:S(2)}) collective-permute-start(bf16[1,8,8,1024]{3,2,1,0:T(8,128)(2,1)S(1)} %slice.150), channel_id=1, source_target_pairs={{0,2},{2,0},{1,3},{3,1},{4,6},{6,4},{5,7},{7,5},{8,10},{10,8},{9,1... | collective-permute-start | bytes 393224 | tf_op jit(solution)/shard_map/ppermute | solution.py:16
  83.1 1.5 collective-permute-start.3
  85.8 0.7 copy-start.15
  99.9 2.6 copy-start.7
  107.3 1.6 copy-start.3
  121.3 236.1 %all-reduce.5.cloned.1.call-start = ((), (), s32[]{:S(2)}) async-start(), calls=%async_computation.7 | async-start | bytes 393216 | tf_op jit(solution)/shard_map/psum | solution.py:256
  147.3 2.8 copy-start.4
  151.4 0.9 copy-start.1
  153.8 4.8 %copy-start.2 = (bf16[4,12,64,64]{2,3,1,0:T(8,128)(2,1)S(1)}, bf16[4,12,64,64]{2,3,1,0:T(8,128)(2,1)}, u32[]{:S(2)}) copy-start(bf16[4,12,64,64]{2,3,1,0:T(8,128)(2,1)} %copy-done.1) | copy-start | bytes 1179652
  160.0 2.9 copy-start.10
  166.3 3.1 copy-start.11
  166.3 3.1 copy-start.12
  173.9 2.7 copy-start.9
  174.0 1.4 collective-permute-start.4
  175.6 17.2 %collective-permute-start.5 = (bf16[1,8,32,1024]{3,2,1,0:T(8,128)(2,1)S(1)}, bf16[1,8,32,1024]{3,2,1,0:T(8,128)(2,1)S(1)}, u32[]{:S(2)}, u32[]{:S(2)}) collective-permute-start(bf16[1,8,32,1024]{3,2,1,0:T(8,128)(2,1)S(1)} %fusion.25), channel_id=1, source_target_pairs={{0,4},{4,8},{8,12},{12,16},{16,20},{20,24},{24,28},{28,0},{1,5},{5... | collective-permute-start | bytes 1572872 | tf_op jit(solution)/shard_map/ppermute | solution.py:16
  192.7 35.0 %copy-start.6 = (f32[12,64,64]{1,2,0:T(8,128)S(1)}, f32[12,64,64]{1,2,0:T(8,128)}, u32[]{:S(2)}) copy-start(f32[12,64,64]{1,2,0:T(8,128)} %get-tuple-element.81) | copy-start | bytes 589828
  193.0 35.0 %copy-start.17 = (s32[4096]{0:T(1024)S(1)}, s32[4096]{0:T(1024)}, u32[]{:S(2)}) copy-start(s32[4096]{0:T(1024)} %copy-done.16) | copy-start | bytes 49156
  193.9 188.1 %reduce-scatter.5.cloned.1.call-start = ((), (), s32[]{:S(2)}) async-start(), calls=%async_computation.5 | async-start | bytes 491520 | tf_op jit(solution)/shard_map/reduce_scatter | solution.py:232
Sparse Core Ops, SparseCore 0:
  10.0 43.0 all-gather.3
  54.7 38.9 all-gather.5
  95.9 43.4 all-gather.7
  142.9 84.6 reduce-scatter.2
  233.6 123.7 all-reduce.4
  360.3 21.7 reduce-scatter.4
where the time goes:
time: 391 us
  waiting for transfers between devices  233 us (60%)
  blocking collectives  52.7 us (13%)
  local copies, waits for them, and re-layouts  38.4 us (10%)
  matrix products  34.1 us (9%)
  between operations  22.4 us (6%)
  other arithmetic  5.59 us (1%)
  starting transfers between devices  4.81 us (1%)
    psum x1, waiting for transfers between devices, on_device(): lax.psum((embed_grad, bias_grad, gain_contribution, table_grad), ('row',...  87.6 us
    all_gather x1, waiting for transfers between devices, on_device(): qkv_rowwise = lax.all_gather(qkv_weight, 'row', axis=0, tiled=True)  45.2 us
    psum x1, blocking collectives, on_device(): lax.psum((embed_grad, bias_grad, gain_contribution, table_grad), ('row',...  40.2 us
    reduce_scatter x1, waiting for transfers between devices, on_device(): lax.psum_scatter(lax.dot_general(attended, cot_flat, (((0,), (0,)), ((),...  33.6 us
    reduce_scatter x1, waiting for transfers between devices, on_device(): lax.psum_scatter(partial_rows, ('col', 'dp'), scatter_dimension=1, tiled=...  24.7 us
    all_gather x1, waiting for transfers between devices, on_device(): lax.all_gather(out_columns, 'row', axis=0, tiled=True)  17.9 us
    ppermute x6, waiting for transfers between devices, from_behind(): return lax.ppermute(value, axis, pairs)  15.7 us
    all_gather x1, blocking collectives, on_device(): lax.all_gather(out_weight, ('col', 'dp'), axis=1, tiled=True)  12.5 us
  transfers between devices with their start and end apart: 12, of which 8 were waited for; matrix products, arithmetic and copies ran while one was open for 19% of the time, Pallas kernels for 0%

commit v1 on v0

--- a/solution.py
+++ b/solution.py
@@ -1,6 +1,10 @@
+import functools
+
 import jax
 import jax.numpy as jnp
 from jax import lax
+from jax.experimental import pallas as pl
+from jax.experimental.pallas import tpu as pltpu
 from jax.sharding import PartitionSpec as P
 
 WIN = 8
@@ -42,28 +46,6 @@
     features = windows.shape[-1]
     shaped = windows.reshape(rows_all // WIN, cols_all // WIN, WIN, WIN, features)
     return shaped.transpose(0, 2, 1, 3, 4).reshape(rows_all, cols_all, features)
-
-
-def splice_after(own_block, borrowed, offsets, along_dim):
-    length = own_block.shape[along_dim]
-
-    def single(own_item, borrowed_item, offset):
-        joined = jnp.concatenate([own_item, borrowed_item], along_dim - 1)
-        return lax.dynamic_slice_in_dim(joined, offset, length, along_dim - 1)
-
-    return jax.vmap(single)(own_block, borrowed, offsets)
-
-
-def splice_before(own_block, borrowed, offsets, along_dim):
-    length = own_block.shape[along_dim]
-    margin = borrowed.shape[along_dim]
-
-    def single(own_item, borrowed_item, offset):
-        joined = jnp.concatenate([borrowed_item, own_item], along_dim - 1)
-        return lax.dynamic_slice_in_dim(joined, margin - offset, length, along_dim - 1)
-
-    return jax.vmap(single)(own_block, borrowed, offsets)
-
 
 def attend_forward(cell_windows, labels, layer_norm_gain, qkv_full, bias_full):
     window_count, cell_count, features = cell_windows.shape
@@ -165,7 +147,363 @@
     return (branch_gradient.astype(jnp.bfloat16), gain_contribution, table_part)
 
 
+MESH = pl.DeviceIdType.MESH
+VMEM = pltpu.VMEM
+
+
+def greet_everyone(sizes, row, col, dp):
+    rows, cols, dps = sizes
+    barrier = pltpu.get_barrier_semaphore()
+    others = 0
+    for r in range(rows):
+        for c in range(cols):
+            for d in range(dps):
+                if r or c or d:
+                    others += 1
+                    pl.semaphore_signal(
+                        barrier,
+                        inc=1,
+                        device_id={
+                            "row": (row + r) % rows,
+                            "col": (col + c) % cols,
+                            "dp": (dp + d) % dps,
+                        },
+                        device_id_type=MESH,
+                    )
+    pl.semaphore_wait(barrier, others)
+
+
+def gather_kernel(
+    sizes, qkv_ref, out_ref, cot_ref, pix_ref,
+    qkv_all, out_all, cot_r, cot_c, cot_x, pix_r, pix_c, pix_x,
+    send_sem, recv_sem, own_sem, halo_send, halo_recv,
+):
+    rows, cols, _ = sizes
+    ring = rows // 2
+    row, col, dp = lax.axis_index("row"), lax.axis_index("col"), lax.axis_index("dp")
+    x, z = row % 2, row // 2
+    greet_everyone(sizes, row, col, dp)
+    gathered = (qkv_all, out_all)
+    own = (qkv_ref, out_ref)
+    started = []
+
+    def slot(array, ident):
+        flag, dy, dx, dz = ident
+        column = (col + flag) % 2
+        which_row = ((z - dz + ring) % ring) * 2 + (x + dx) % 2
+        return gathered[array].at[column * 2 + (dp + dy) % 2, which_row]
+
+    def semaphore(array, ident):
+        flag, dy, dx, dz = ident
+        return recv_sem.at[array, ((flag * 2 + dy) * 2 + dx) * ring + dz]
+
+    def send(ident, device, landing):
+        for array in range(2):
+            source = own[array] if ident == (0, 0, 0, 0) else slot(array, ident)
+            copy = pltpu.make_async_remote_copy(
+                src_ref=source,
+                dst_ref=slot(array, ident),
+                send_sem=send_sem.at[len(started)],
+                recv_sem=semaphore(array, landing),
+                device_id=device,
+                device_id_type=MESH,
+            )
+            copy.start()
+            started.append(copy)
+
+    def arrive(ident):
+        for array in range(2):
+            pltpu.make_async_remote_copy(
+                src_ref=slot(array, ident),
+                dst_ref=slot(array, ident),
+                send_sem=send_sem.at[0],
+                recv_sem=semaphore(array, ident),
+                device_id={"col": (col + 1) % 2},
+                device_id_type=MESH,
+            ).wait_recv()
+
+    over_y = {"dp": (dp + 1) % 2}
+    over_x = {"row": z * 2 + (x + 1) % 2}
+    up = {"row": ((z + 1) % ring) * 2 + x}
+    down = {"row": ((z + ring - 1) % ring) * 2 + x}
+    over_core = {"col": (col + 1) % 2}
+
+    def onward_up(dy, dx, dz):
+        if dz + 1 < ring // 2 or (dz + 1 == ring // 2 and dy == 0):
+            send((0, dy, dx, dz), up, (0, dy, dx, dz + 1))
+
+    def onward_down(dy, dx, back):
+        if back + 1 < ring // 2 or (back + 1 == ring // 2 and dy == 1):
+            send((0, dy, dx, (ring - back) % ring), down, (0, dy, dx, ring - back - 1))
+
+    def spread(dy, dx):
+        onward_up(dy, dx, 0)
+        onward_down(dy, dx, 0)
+
+    send((0, 0, 0, 0), over_y, (0, 1, 0, 0))
+    send((0, 0, 0, 0), over_x, (0, 0, 1, 0))
+    spread(0, 0)
+    send((0, 0, 0, 0), over_core, (1, 0, 0, 0))
+    local = [
+        pltpu.make_async_copy(own[array], slot(array, (0, 0, 0, 0)), own_sem.at[array])
+        for array in range(2)
+    ]
+    for copy in local:
+        copy.start()
+    arrive((0, 1, 0, 0))
+    send((0, 1, 0, 0), over_x, (0, 1, 1, 0))
+    spread(1, 0)
+    above = (row + rows - 1) % rows
+    left = (col + cols - 1) % cols
+    edge = cot_c.shape[1]
+    halos = []
+    for source, target, device in (
+        (pix_ref, pix_r, {"row": above}),
+        (pix_ref, pix_c, {"col": left}),
+        (pix_ref, pix_x, {"row": above, "col": left}),
+        (cot_ref, cot_r, {"row": above}),
+        (cot_ref.at[:, pl.ds(0, edge)], cot_c, {"col": left}),
+        (cot_ref.at[:, pl.ds(0, edge)], cot_x, {"row": above, "col": left}),
+    ):
+        copy = pltpu.make_async_remote_copy(
+            src_ref=source,
+            dst_ref=target,
+            send_sem=halo_send.at[len(halos)],
+            recv_sem=halo_recv.at[len(halos)],
+            device_id=device,
+            device_id_type=MESH,
+        )
+        copy.start()
+        halos.append(copy)
+    send((0, 1, 0, 0), over_core, (1, 1, 0, 0))
+    for dy in range(2):
+        arrive((0, dy, 1, 0))
+        spread(dy, 1)
+        send((0, dy, 1, 0), over_core, (1, dy, 1, 0))
+    for step in range(1, ring // 2 + 1):
+        for dx in range(2):
+            for dy in range(2):
+                if step < ring // 2 or dy == 0:
+                    arrive((0, dy, dx, step))
+                    onward_up(dy, dx, step)
+                    send((0, dy, dx, step), over_core, (1, dy, dx, step))
+                if step < ring // 2 or dy == 1:
+                    arrive((0, dy, dx, ring - step))
+                    onward_down(dy, dx, step)
+                    send((0, dy, dx, ring - step), over_core, (1, dy, dx, ring - step))
+    for dz in range(ring):
+        for dx in range(2):
+            for dy in range(2):
+                arrive((1, dy, dx, dz))
+    for copy in halos:
+        copy.wait_recv()
+    for copy in started + halos:
+        copy.wait_send()
+    for copy in local:
+        copy.wait()
+
+
+def gather_inputs(sizes, qkv_weight, out_weight, cot_block, pix_block):
+    rows, cols, dps = sizes
+    groups = cols * dps
+    edge = (cot_block.shape[0], WIN, cot_block.shape[2])
+    cot_type, pix_type = cot_block.dtype, pix_block.dtype
+    shapes = [
+        ((groups, rows) + qkv_weight.shape, qkv_weight.dtype),
+        ((groups, rows) + out_weight.shape, out_weight.dtype),
+        (cot_block.shape, cot_type),
+        (edge, cot_type),
+        (edge, cot_type),
+        (pix_block.shape, pix_type),
+        (pix_block.shape, pix_type),
+        (pix_block.shape, pix_type),
+    ]
+    return pl.pallas_call(
+        functools.partial(gather_kernel, sizes),
+        out_shape=[jax.ShapeDtypeStruct(shape, kind) for shape, kind in shapes],
+        in_specs=[pl.BlockSpec(memory_space=VMEM)] * 4,
+        out_specs=[pl.BlockSpec(memory_space=VMEM)] * 8,
+        scratch_shapes=[
+            pltpu.SemaphoreType.DMA((4 * rows * groups,)),
+            pltpu.SemaphoreType.DMA((2, rows * groups)),
+            pltpu.SemaphoreType.DMA((2,)),
+            pltpu.SemaphoreType.DMA((6,)),
+            pltpu.SemaphoreType.DMA((6,)),
+        ],
+        compiler_params=pltpu.CompilerParams(
+            collective_id=0, has_side_effects=True, vmem_limit_bytes=40 * 2**20
+        ),
+        name="gather_inputs",
+    )(qkv_weight, out_weight, cot_block, pix_block)
+
+
+def reduce_kernel(
+    sizes, grad_ref, small_ref, grad_out, small_out,
+    core_g, core_e, made_g, made_e, z_g, z_e, acc_g, acc_e,
+    xs_g, xs_e, x_g, x_e, ys_g, y_g, ys_e, y_e, tot_e,
+    core_send, core_recv, z_send, z_recv, xy_send, xy_recv, all_send, all_recv,
+):
+    rows, cols, dps = sizes
+    ring = rows // 2
+    row, col, dp = lax.axis_index("row"), lax.axis_index("col"), lax.axis_index("dp")
+    x, z = row % 2, row // 2
+    f32, low = jnp.float32, jnp.bfloat16
+    greet_everyone(sizes, row, col, dp)
+    other = (col + 1) % 2
+
+    def remote(source, target, send_sem, recv_sem, device):
+        copy = pltpu.make_async_remote_copy(
+            src_ref=source, dst_ref=target, send_sem=send_sem, recv_sem=recv_sem,
+            device_id=device, device_id_type=MESH,
+        )
+        copy.start()
+        return copy
+
+    order = [ring // 2] + [s for s in range(1, ring) if s != ring // 2] + [0]
+    across = {}
+    for s in order:
+        there = ((z + s) % ring) * 2
+        across[s] = [
+            remote(
+                source.at[pl.ds(other * 2, 2), pl.ds(there, 2)], target.at[s],
+                core_send.at[i, s], core_recv.at[i, s], {"col": other},
+            )
+            for i, (source, target) in enumerate(((grad_ref, core_g), (small_ref, core_e)))
+        ]
+    sent = []
+    for s in order:
+        for copy in across[s]:
+            copy.wait_recv()
+        there = ((z + s) % ring) * 2
+        for d in range(2):
+            for h in range(2):
+                total = grad_ref[col * 2 + d, there + h].astype(f32) + core_g[s, d, h].astype(f32)
+                small = small_ref[col * 2 + d, there + h] + core_e[s, d, h]
+                if s:
+                    made_g[s, d, h] = total.astype(low)
+                    made_e[s, d, h] = small
+                else:
+                    acc_g[d, h] = total
+                    acc_e[d, h] = small
+        if s:
+            device = {"row": there + x}
+            sent.append(remote(made_g.at[s], z_g.at[s], z_send.at[0, s], z_recv.at[0, s], device))
+            sent.append(remote(made_e.at[s], z_e.at[s], z_send.at[1, s], z_recv.at[1, s], device))
+    for copy in sent:
+        copy.wait_recv()
+
+    def z_sum(d, h):
+        total, small = acc_g[d, h], acc_e[d, h]
+        for s in range(1, ring):
+            total = total + z_g[s, d, h].astype(f32)
+            small = small + z_e[s, d, h]
+        return total, small
+
+    away = (x + 1) % 2
+    for d in range(2):
+        total, small = z_sum(d, away)
+        xs_g[d] = total.astype(low)
+        xs_e[d] = small
+    device = {"row": z * 2 + away}
+    pair = [
+        remote(xs_g, x_g, xy_send.at[0], xy_recv.at[0], device),
+        remote(xs_e, x_e, xy_send.at[1], xy_recv.at[1], device),
+    ]
+    mine, mine_small = z_sum(dp, x)
+    far, far_small = z_sum((dp + 1) % 2, x)
+    for copy in pair:
+        copy.wait_recv()
+    ys_g[...] = (far + x_g[(dp + 1) % 2].astype(f32)).astype(low)
+    ys_e[...] = far_small + x_e[(dp + 1) % 2]
+    device = {"dp": (dp + 1) % 2}
+    last = [
+        remote(ys_e, y_e, xy_send.at[3], xy_recv.at[3], device),
+        remote(ys_g, y_g, xy_send.at[2], xy_recv.at[2], device),
+    ]
+    mine = mine + x_g[dp].astype(f32)
+    mine_small = mine_small + x_e[dp]
+    last[0].wait_recv()
+    group = col * 2 + dp
+    whole = mine_small + y_e[...]
+    tot_e[...] = whole
+    spread = []
+    for r in range(rows):
+        for c in range(cols):
+            for d in range(dps):
+                if r or c or d:
+                    index = (r * cols + c) * dps + d
+                    spread.append(
+                        remote(
+                            tot_e, small_out.at[group, row],
+                            all_send.at[index], all_recv.at[index],
+                            {
+                                "row": (row + r) % rows,
+                                "col": (col + c) % cols,
+                                "dp": (dp + d) % dps,
+                            },
+                        )
+                    )
+    small_out[group, row] = whole
+    last[1].wait_recv()
+    grad_out[...] = mine + y_g[...].astype(f32)
+    index = 0
+    for r in range(rows):
+        for c in range(cols):
+            for d in range(dps):
+                if r or c or d:
+                    place = (r * cols + c) * dps + d
+                    source_group = ((col + cols - c) % cols) * dps + (dp + dps - d) % dps
+                    pltpu.make_async_remote_copy(
+                        src_ref=tot_e,
+                        dst_ref=small_out.at[source_group, (row + rows - r) % rows],
+                        send_sem=all_send.at[place],
+                        recv_sem=all_recv.at[place],
+                        device_id={"col": other},
+                        device_id_type=MESH,
+                    ).wait_recv()
+    for s in order:
+        for copy in across[s]:
+            copy.wait_send()
+    for copy in sent + pair + last + spread:
+        copy.wait_send()
+
+
+def reduce_outputs(sizes, grad_blocks, small_blocks):
+    rows, cols, dps = sizes
+    ring = rows // 2
+    big, tiny = grad_blocks.shape[2:], small_blocks.shape[2:]
+    f32, low = jnp.float32, jnp.bfloat16
+    dma = pltpu.SemaphoreType.DMA
+    return pl.pallas_call(
+        functools.partial(reduce_kernel, sizes),
+        out_shape=[
+            jax.ShapeDtypeStruct(big, f32),
+            jax.ShapeDtypeStruct(small_blocks.shape, f32),
+        ],
+        in_specs=[pl.BlockSpec(memory_space=VMEM)] * 2,
+        out_specs=[pl.BlockSpec(memory_space=VMEM)] * 2,
+        scratch_shapes=[
+            VMEM((ring, 2, 2) + big, low), VMEM((ring, 2, 2) + tiny, f32),
+            VMEM((ring, 2, 2) + big, low), VMEM((ring, 2, 2) + tiny, f32),
+            VMEM((ring, 2, 2) + big, low), VMEM((ring, 2, 2) + tiny, f32),
+            VMEM((2, 2) + big, f32), VMEM((2, 2) + tiny, f32),
+            VMEM((2,) + big, low), VMEM((2,) + tiny, f32),
+            VMEM((2,) + big, low), VMEM((2,) + tiny, f32),
+            VMEM(big, low), VMEM(big, low), VMEM(tiny, f32), VMEM(tiny, f32), VMEM(tiny, f32),
+            dma((2, ring)), dma((2, ring)), dma((2, ring)), dma((2, ring)),
+            dma((4,)), dma((4,)),
+            dma((rows * cols * dps,)), dma((rows * cols * dps,)),
+        ],
+        compiler_params=pltpu.CompilerParams(
+            collective_id=1, has_side_effects=True, vmem_limit_bytes=40 * 2**20
+        ),
+        name="reduce_outputs",
+    )(grad_blocks, small_blocks)
+
+
 def on_device(
+    direct,
+    sizes,
     pixels,
     cotangent,
     embed_weight,
@@ -178,88 +516,132 @@
     shifts,
 ):
     images, rows_dev, cols_dev, features = cotangent.shape
-    head_count = bias_table.shape[0]
-    grid_rows = rows_dev * lax.axis_size("row")
-    grid_cols = cols_dev * lax.axis_size("col")
-    row_shift = shifts[:, 0]
-    col_shift = shifts[:, 1]
-    qkv_rowwise = lax.all_gather(qkv_weight, "row", axis=0, tiled=True)
-    qkv_full, out_columns = (
-        lax.all_gather(qkv_rowwise, ("col", "dp"), axis=1, tiled=True),
-        lax.all_gather(out_weight, ("col", "dp"), axis=1, tiled=True),
-    )
-    patches = make_patches(pixels)
-    tokens = embed_cells(patches, embed_weight, embed_bias)
-    below = from_behind((tokens, cotangent), "row", -1)
-    shifted = splice_after(tokens, below[0], row_shift, 1)
-    shifted_cot = splice_after(cotangent, below[1], row_shift, 1)
-    beside = from_behind((shifted[:, :, :WIN], shifted_cot[:, :, :WIN]), "col", -1)
-    shifted = splice_after(shifted, beside[0], col_shift, 2)
-    shifted_cot = splice_after(shifted_cot, beside[1], col_shift, 2)
+    rows, cols, dps = sizes
+    head_count, table_size = bias_table.shape
+    pix_block, cot_block = pixels[0], cotangent[0]
+    row_shift, col_shift = shifts[0, 0], shifts[0, 1]
+    if direct:
+        qkv_all, out_all, cot_r, cot_c, cot_x, pix_r, pix_c, pix_x = gather_inputs(
+            sizes, qkv_weight, out_weight, cot_block, pix_block
+        )
+        qkv_full = jnp.concatenate(
+            [w.reshape(-1, qkv_weight.shape[1]) for w in qkv_all], axis=1
+        )
+        out_full = jnp.concatenate(
+            [w.reshape(-1, out_weight.shape[1]) for w in out_all], axis=1
+        )
+    else:
+        qkv_full, out_full = [
+            lax.all_gather(
+                lax.all_gather(w, "row", axis=0, tiled=True), ("col", "dp"), axis=1, tiled=True
+            )
+            for w in (qkv_weight, out_weight)
+        ]
+        pix_r, cot_r = from_behind((pix_block, cot_block), "row", -1)
+        pix_c, cot_c = from_behind((pix_block, cot_block[:, :WIN]), "col", -1)
+        pix_x, cot_x = from_behind((pix_c, cot_c), "row", -1)
+    wide_pix = jnp.concatenate(
+        [
+            jnp.concatenate([pix_block, pix_c[:, :, : WIN * PATCH]], axis=2),
+            jnp.concatenate([pix_r, pix_x[:, :, : WIN * PATCH]], axis=2),
+        ],
+        axis=1,
+    )
+    wide_cot = jnp.concatenate(
+        [
+            jnp.concatenate([cot_block, cot_c], axis=1),
+            jnp.concatenate([cot_r, cot_x], axis=1),
+        ],
+        axis=0,
+    )
+    wide_patches = make_patches(wide_pix[None])[0]
+    patches = lax.dynamic_slice(
+        wide_patches, (row_shift, col_shift, 0), (rows_dev, cols_dev, wide_patches.shape[2])
+    )
+    shifted_cot = lax.dynamic_slice(
+        wide_cot, (row_shift, col_shift, 0), (rows_dev, cols_dev, features)
+    )
+    patch_rows = window_split(patches).reshape(-1, patches.shape[2])
+    cot_flat = window_split(shifted_cot).reshape(-1, features)
+    grid_rows, grid_cols = rows_dev * rows, cols_dev * cols
     row_ids = lax.axis_index("row") * rows_dev + jnp.arange(rows_dev, dtype=jnp.int32)
     col_ids = lax.axis_index("col") * cols_dev + jnp.arange(cols_dev, dtype=jnp.int32)
-    row_part = (row_ids[None, :] >= grid_rows - row_shift[:, None]).astype(jnp.int32)
-    col_part = (col_ids[None, :] >= grid_cols - col_shift[:, None]).astype(jnp.int32)
-    region = 2 * row_part[:, :, None] + col_part[:, None, :]
-    labels = window_split(region.reshape(images * rows_dev, cols_dev, 1))[:, :, 0]
-    cell_windows = window_split(shifted.reshape(images * rows_dev, cols_dev, features))
-    cot_flat = window_split(shifted_cot.reshape(images * rows_dev, cols_dev, features)).reshape(
-        -1, features
-    )
+    row_part = (row_ids >= grid_rows - row_shift).astype(jnp.int32)
+    col_part = (col_ids >= grid_cols - col_shift).astype(jnp.int32)
+    region = 2 * row_part[:, None] + col_part[None, :]
+    labels = window_split(region[:, :, None])[:, :, 0]
     selector = (
-        rel_index.reshape(-1)[:, None] == jnp.arange(bias_table.shape[1], dtype=jnp.int32)[None, :]
+        rel_index.reshape(-1)[:, None] == jnp.arange(table_size, dtype=jnp.int32)[None, :]
     ).astype(jnp.float32)
     bias_full = jnp.dot(selector, bias_table.T, precision=lax.Precision.HIGHEST).T.reshape(
         head_count, WIN * WIN, WIN * WIN
     )
+    cells = embed_cells(patch_rows, embed_weight, embed_bias)
     stored_residuals, attended = attend_forward(
-        cell_windows, labels, layer_norm_gain, qkv_full, bias_full
+        cells.reshape(-1, WIN * WIN, features), labels, layer_norm_gain, qkv_full, bias_full
     )
     d_attended = lax.dot_general(
-        cot_flat,
-        lax.all_gather(out_columns, "row", axis=0, tiled=True),
-        (((1,), (1,)), ((), ())),
-        preferred_element_type=jnp.float32,
+        cot_flat, out_full, (((1,), (1,)), ((), ())), preferred_element_type=jnp.float32
     ).astype(jnp.bfloat16)
-    partial_rows = lax.psum_scatter(
-        lax.dot_general(
-            attended, cot_flat, (((0,), (0,)), ((), ())), preferred_element_type=jnp.float32
-        ),
-        "row",
-        scatter_dimension=0,
-        tiled=True,
-    )
-    out_weight_grad = lax.psum_scatter(partial_rows, ("col", "dp"), scatter_dimension=1, tiled=True)
     d_rows, gain_contribution, table_part = attend_backward(
         stored_residuals, d_attended, layer_norm_gain, qkv_full
     )
-    branch_gradient = window_join(
-        d_rows.reshape(-1, WIN * WIN, features), images * rows_dev, cols_dev
-    ).reshape(images, rows_dev, cols_dev, features)
-    patch_rows = patches.reshape(-1, patches.shape[-1])
-    cot_rows = cotangent.reshape(-1, features)
-    contract = (((0,), (0,)), ((), ()))
-    behind = from_behind(branch_gradient[:, :, cols_dev - WIN :], "col", 1)
-    d_back = splice_before(branch_gradient, behind, col_shift, 2)
-    above = from_behind(d_back, "row", 1)
-    d_back = splice_before(d_back, above, row_shift, 1)
-    back_rows = d_back.reshape(-1, features)
-    embed_grad = lax.dot_general(
-        patch_rows, cot_rows, contract, preferred_element_type=jnp.float32
-    ) + lax.dot_general(patch_rows, back_rows, contract, preferred_element_type=jnp.float32)
-    bias_grad = jnp.sum(cot_rows, axis=0, dtype=jnp.float32) + jnp.sum(
-        back_rows, axis=0, dtype=jnp.float32
-    )
     table_grad = jnp.dot(
         table_part.reshape(head_count, -1), selector, precision=lax.Precision.HIGHEST
     )
-    totals = lax.psum((embed_grad, bias_grad, gain_contribution, table_grad), ("row", "col", "dp"))
-    return (out_weight_grad, totals[0], totals[1], totals[2], totals[3])
+    contract = (((0,), (0,)), ((), ()))
+    back_rows = jnp.concatenate([cot_flat, d_rows], axis=0)
+    embed_grad = lax.dot_general(
+        jnp.concatenate([patch_rows, patch_rows], axis=0),
+        back_rows,
+        contract,
+        preferred_element_type=jnp.float32,
+    )
+    bias_grad = jnp.sum(back_rows, axis=0, dtype=jnp.float32)
+    if not direct:
+        partial_rows = lax.psum_scatter(
+            lax.dot_general(attended, cot_flat, contract, preferred_element_type=jnp.float32),
+            "row",
+            scatter_dimension=0,
+            tiled=True,
+        )
+        out_weight_grad = lax.psum_scatter(
+            partial_rows, ("col", "dp"), scatter_dimension=1, tiled=True
+        )
+        totals = lax.psum(
+            (embed_grad, bias_grad, gain_contribution, table_grad), ("row", "col", "dp")
+        )
+        return (out_weight_grad,) + totals
+    groups = cols * dps
+    cot_groups = cot_flat.reshape(-1, groups, features // groups)
+    grad_blocks = jnp.stack(
+        [
+            lax.dot_general(
+                attended, cot_groups[:, k], contract, preferred_element_type=jnp.float32
+            ).astype(jnp.bfloat16)
+            for k in range(groups)
+        ]
+    ).reshape((groups, rows) + out_weight.shape)
+    pieces = (embed_grad, bias_grad, gain_contribution, table_grad)
+    flat = jnp.concatenate([piece.reshape(-1) for piece in pieces])
+    unit = groups * rows * 2048
+    flat = jnp.pad(flat, (0, -flat.shape[0] % unit))
+    out_weight_grad, small = reduce_outputs(
+        sizes, grad_blocks, flat.reshape(groups, rows, -1, 256)
+    )
+    small = small.reshape(-1)
+    totals, start = [], 0
+    for piece in pieces:
+        totals.append(small[start : start + piece.size].reshape(piece.shape))
+        start += piece.size
+    return (out_weight_grad,) + tuple(totals)
 
 
 def solution(mesh):
+    sizes = tuple(mesh.shape[name] for name in ("row", "col", "dp"))
+    direct = sizes[1:] == (2, 2) and sizes[0] == 8
     return jax.shard_map(
-        on_device,
+        functools.partial(on_device, direct, sizes),
         mesh=mesh,
         in_specs=(
             P("dp", None, "row", "col"),

time: 391 us -> 204 us (0.52)
  waiting for transfers between devices: 233 us -> 0 us
  Pallas kernels: 0 us -> 121 us
  blocking collectives: 52.7 us -> 0 us
  between operations: 22.4 us -> 6.44 us
  matrix products: 34.1 us -> 25.7 us
  local copies, waits for them, and re-layouts: 38.4 us -> 43.5 us
  starting transfers between devices: 4.81 us -> 0 us
    pallas_call x0 -> x2, Pallas kernels: none -> 121 us  [the longest x1 81.5 us: gather_inputs(): pl.pallas_call(functools.partial(gather_kernel, sizes), out_shape=[jax.Sh...]
    psum x1 -> x0, waiting for transfers between devices: 87.6 us -> none  [on_device(): lax.psum((embed_grad, bias_grad, gain_contribution, table_grad), ('row',...]
    all_gather x3 -> x0, waiting for transfers between devices: 70.1 us -> none  [the longest x1 45.2 us: on_device(): qkv_rowwise = lax.all_gather(qkv_weight, 'row', axis=0, tiled=True)]
    reduce_scatter x2 -> x0, waiting for transfers between devices: 58.3 us -> none  [the longest x1 33.6 us: on_device(): lax.psum_scatter(lax.dot_general(attended, cot_flat, (((0,), (0,)), ((),...]
    psum x1 -> x0, blocking collectives: 40.2 us -> none  [on_device(): lax.psum((embed_grad, bias_grad, gain_contribution, table_grad), ('row',...]
    ppermute x6 -> x0, waiting for transfers between devices: 15.7 us -> none  [from_behind(): return lax.ppermute(value, axis, pairs)]
    all_gather x1 -> x0, blocking collectives: 12.5 us -> none  [on_device(): lax.all_gather(out_weight, ('col', 'dp'), axis=1, tiled=True)]
    concatenate x0 -> x1, local copies, waits for them, and re-layouts: none -> 8.12 us  [on_device(): jnp.concatenate([w.reshape(-1, qkv_weight.shape[1]) for w in qkv_all], ax...]
  transfers between devices with their start and end apart: 12 -> 0, of which waited for: 8 -> 0; matrix products, arithmetic and copies ran while one was open for 19% -> 0% of each run, Pallas kernels for 0% -> 0%
where the time goes in v1:
time: 204 us; the launch traced here: 203 us
  Pallas kernels  121 us (59%)
  local copies, waits for them, and re-layouts  43.5 us (21%)
  matrix products  25.7 us (13%)
  other arithmetic  6.65 us (3%)
  between operations  6.44 us (3%)
    pallas_call x1, Pallas kernels, gather_inputs(): pl.pallas_call(functools.partial(gather_kernel, sizes), out_shape=[jax.Sh...  81.5 us
    pallas_call x1, Pallas kernels, reduce_outputs(): pl.pallas_call(functools.partial(reduce_kernel, sizes), out_shape=[jax.Sh...  39.3 us
    concatenate x1, local copies, waits for them, and re-layouts, on_device(): jnp.concatenate([w.reshape(-1, qkv_weight.shape[1]) for w in qkv_all], ax...  8.12 us
    unnamed x60, local copies, waits for them, and re-layouts  5.58 us
    another operation x1, local copies, waits for them, and re-layouts, on_device(): qkv_full = jnp.concatenate([w.reshape(-1, qkv_weight.shape[1]) for w in q...  4.62 us
    dot_general x1, matrix products, attend_backward(): jnp.einsum('whmn,wmhd->wnhd', reduced_probability, d_heads, preferred_ele...  4.13 us

profile of v1, /device:TPU:0, one launch (start us, length us, event | category | flops | bytes accessed | tf_op | source)
XLA Modules:
  0.0 203.1 jit_solution(4224717791583351686)
XLA Ops:
  0.7 1.3 fusion.76
  7.4 0.8 eq.39
  8.3 1.1 copy.117.qkv_ref
  9.4 2.7 %convolution_bitcast_fusion = f32[12,4096]{1,0:T(8,128)S(1)} fusion(f32[12,225]{1,0:T(8,128)} %param.17, s32[4096]{0:T(1024)S(1)} %eq.39), kind=kOutput, calls=%fused_computation.1 | convolution fusion | flops 133632000 | bytes 223792 | tf_op jit(solution)/shard_map/dot_general | solution.py:576
  12.1 0.2 add.93
  12.3 0.9 copy.126
  13.2 81.5 %gather_inputs.1 = (bf16[4,8,128,576]{3,2,1,0:T(8,128)(2,1)S(1)}, bf16[4,8,96,256]{3,2,1,0:T(8,128)(2,1)S(1)}, bf16[8,32,1024]{2,1,0:T(8,128)(2,1)S(1)}, bf16[8,...) custom-call(bf16[128,576]{1,0:T(8,128)(2,1)S(1)} %copy.117.qkv_ref, ...), custom_call_target="tpu_custom_call" | custom-call | tf_op jit(solution)/shard_map/gather_inputs/pallas_call | solution.py:321
  94.7 2.3 %copy-done.1 = bf16[4,8,128,576]{3,2,1,0:T(8,128)(2,1)} copy-done((bf16[4,8,128,576]{3,2,1,0:T(8,128)(2,1)}, bf16[4,8,128,576]{3,2,1,0:T(8,128)(2,1)S(1)}, u32[]{:S(2)}) %copy-start.1) | copy-done | bytes 4718616
  97.0 1.1 fusion.49
  98.2 0.4 reshape_reshape_reshape.3
  98.5 1.8 fusion.74
  100.3 0.1 fusion.72
  100.5 0.6 fusion.19
  101.1 0.6 reshape.158
  101.7 1.5 copy.145
  103.3 1.3 reshape_broadcast_in_dim.4
  104.6 1.6 copy.118
  106.4 0.7 copy.131
  107.1 0.4 convert_reduce_fusion.1
  107.5 0.3 fusion.40
  107.8 4.6 %fusion.71 = (bf16[1,8,128,576]{3,2,1,0:T(8,128)(2,1)S(1)}, bf16[1,8,128,576]{3,2,1,0:T(8,128)(2,1)S(1)}, bf16[1,8,128,576]{3,2,1,0:T(8,128)(2,1)}, bf16[1,8,128,576]{3,2,1,0:T(8,128)(2,1)}) fusion(bf16[4,8,128,576]{3,2,1,0:T(8,128)(2,1)} %copy-done.1), kind=kLoop, calls=%fused_computation.109 | loop fusion | bytes 9437184 | tf_op jit(solution)/shard_map/unstack | solution.py:528
  112.4 8.1 %concatenate.40 = bf16[1024,2304]{1,0:T(8,128)(2,1)} concatenate(bf16[1024,576]{1,0:T(8,128)(2,1)} %bitcast.107, bf16[1024,576]{1,0:T(8,128)(2,1)} %bitcast.106, bf16[1024,576]{1,0:T(8,128)(2,1)S(1)} %bitcast.105, bf16[1024,576]{1,0:T(8,128)(2,1)S(1)} %bitcast.104), dimensions={1} | concatenate | bytes 9437184 | tf_op jit(solution)/shard_map/concatenate | solution.py:527
  120.6 3.8 %convolution_convert_fusion = bf16[256,2304]{1,0:T(8,128)(2,1)S(1)} fusion(bf16[1024,2304]{1,0:T(8,128)(2,1)} %concatenate.40, bf16[256,1024]{1,0:T(8,128)(2,1)S(1)} %get-tuple-element.50, f32[1024]{0:T(1024)S(1)} %copy-done.23, f32[256]{0:T(256)S(1)} %add_rsqrt_fusion, f32[256]{0:T(256)S(1)} %broadcast_multiply_fusion.2), kind=kOutput, calls=%fused_computation.4 | convolution fusion | flops 1209860096 | bytes 6428672 | tf_op jit(solution)/shard_map/dot_general | solution.py:64
  124.5 0.6 reshape.157
  125.1 0.9 copy.137
  126.0 1.7 reshape.155
  127.6 0.6 reshape.156
  128.3 1.1 copy.141
  129.4 0.4 add_select_fusion
  129.8 2.4 %fusion.77 = (f32[4,12,64]{2,1,0:T(8,128)S(1)}, f32[4,12,64,64]{2,3,1,0:T(8,128)S(1)}) fusion(f32[4,12,64,64]{2,3,1,0:T(8,128)S(1)} %add_select_fusion), kind=kOutput, calls=%fused_computation.115 | output fusion | flops 393279 | bytes 1585152 | tf_op jit(solution)/shard_map/sub | solution.py:79
  132.2 4.1 %fusion.16 = bf16[4,64,12,64]{1,3,2,0:T(8,128)(2,1)} fusion(bf16[4,64,12,64]{1,3,2,0:T(8,128)(2,1)} %copy.145, f32[4,12,64]{2,1,0:T(8,128)S(1)} %get-tuple-element.51, f32[4,12,64,64]{2,3,1,0:T(8,128)} %copy-done.6), kind=kOutput, calls=%fused_computation.35 | convolution fusion | flops 25955392 | bytes 1585152 | tf_op jit(solution)/shard_map/whmn,wmhd->wnhd/dot_general | solution.py:113
  136.3 3.7 %fusion.15 = bf16[4,64,12,64]{1,3,2,0:T(8,128)(2,1)} fusion(bf16[4,64,12,64]{3,2,1,0:T(8,128)(2,1)} %reshape.155, f32[4,12,64]{2,1,0:T(8,128)S(1)} %get-tuple-element.51, f32[4,12,64,64]{2,3,1,0:T(8,128)} %copy-done.6), kind=kOutput, calls=%fused_computation.34 | convolution fusion | flops 25955392 | bytes 1585152 | tf_op jit(solution)/shard_map/whmn,wnhd->wmhd/dot_general | solution.py:82
  140.1 1.9 multiply_reduce_fusion
  142.0 1.9 fusion.42
  144.0 0.2 copy.148
  144.1 0.1 reshape.149
  144.3 1.4 fusion.1
  145.8 0.5 fusion.18
  146.3 0.6 fusion.17
  146.9 0.6 copy.140
  147.5 1.2 reshape.145
  148.8 0.8 copy.144
  149.6 1.3 reshape.146
  150.9 0.6 copy.129
  151.5 0.5 reshape.142
  152.1 0.6 copy.147
  152.7 0.5 reshape.147
  153.3 4.1 %fusion.35 = (f32[256]{0:T(256)S(1)}, f32[1024]{0:T(1024)S(1)}, f32[256]{0:T(256)S(1)}, f32[256,1024]{1,0:T(8,128)S(1)}) fusion(bf16[256,1024]{1,0:T(8,128)(2,1)S(1)} %copy-done.10, f32[1024]{0:T(1024)S(1)} %copy-done.24, f32[256]{0:T(256)S(1)} %copy-done.26, f32[256]{0:T(256)S(1)} %copy-done.22, bf16[1024,2304]{1,0:T(8,128)(2,1)} %concatenate.40, ...), kind=kOutput, calls=%fused_computation.57 | convolution fusion | flops 1213856256 | bytes 7483392 | tf_op jit(solution)/shard_map/dot_general | solution.py:137
  157.4 0.4 fusion.38
  157.8 0.6 copy-done.8
  158.4 0.2 convert_reduce_fusion
  158.6 0.3 convolution_bitcast_fusion.1
  159.1 0.5 copy-done.17
  159.6 0.3 convolution_convert_fusion.3
  159.9 0.3 convolution_convert_fusion.4
  160.2 0.3 convolution_convert_fusion.5
  160.5 0.3 convolution_convert_fusion.6
  160.7 0.2 pad_maximum_fusion.grad_ref
  160.9 39.3 %reduce_outputs.1 = (f32[96,256]{1,0:T(8,128)S(1)}, f32[4,8,8,256]{3,2,1,0:T(8,128)S(1)}) custom-call(bf16[4,8,96,256]{3,2,1,0:T(8,128)(2,1)S(1)} %pad_maximum_fusion.grad_ref, f32[4,8,8,256]{3,2,1,0:T(8,128)S(1)} %reshape.151.small_ref), custom_call_target="tpu_custom_call" | custom-call | tf_op jit(solution)/shard_map/reduce_outputs/pallas_call | solution.py:477
  200.3 0.7 reshape.152
  201.0 0.1 copy.168
  201.2 0.6 fusion.75
  201.8 0.7 reshape.154
  202.5 0.6 copy.192
  (73 shorter events, 1.2 us)
Async XLA Ops:
  0.6 106.5 %copy-start = (bf16[48,1024]{1,0:T(8,128)(2,1)S(1)}, bf16[48,1024]{1,0:T(8,128)(2,1)}, u32[]{:S(2)}) copy-start(bf16[48,1024]{1,0:T(8,128)(2,1)} %param.12) | copy-start | bytes 294916
  0.6 12.5 %copy-start.4 = (bf16[96,256]{1,0:T(8,128)(2,1)S(1)}, bf16[96,256]{1,0:T(8,128)(2,1)}, u32[]{:S(2)}) copy-start(bf16[96,256]{1,0:T(8,128)(2,1)} %out_ref.1) | copy-start | bytes 147460
  0.7 12.5 %copy-start.2 = (bf16[1,8,32,1024]{3,2,1,0:T(8,128)(2,1)S(1)}, bf16[1,8,32,1024]{3,2,1,0:T(8,128)(2,1)}, u32[]{:S(2)}) copy-start(bf16[1,8,32,1024]{3,2,1,0:T(8,128)(2,1)} %param.11) | copy-start | bytes 1572868
  0.7 12.5 %copy-start.3 = (bf16[1,3,32,128]{3,2,1,0:T(8,128)(2,1)S(1)}, bf16[1,3,32,128]{3,2,1,0:T(8,128)(2,1)}, u32[]{:S(2)}) copy-start(bf16[1,3,32,128]{3,2,1,0:T(8,128)(2,1)} %param.10) | copy-start | bytes 73732
  94.7 2.3 %copy-start.1 = (bf16[4,8,128,576]{3,2,1,0:T(8,128)(2,1)}, bf16[4,8,128,576]{3,2,1,0:T(8,128)(2,1)S(1)}, u32[]{:S(2)}) copy-start(bf16[4,8,128,576]{3,2,1,0:T(8,128)(2,1)S(1)} %get-tuple-element.18) | copy-start | bytes 14155780
  98.1 2.3 %copy-start.7 = (bf16[1,4,8,8,1024]{4,3,2,1,0:T(8,128)(2,1)}, bf16[1,4,8,8,1024]{4,3,2,1,0:T(8,128)(2,1)S(1)}, u32[]{:S(2)}) copy-start(bf16[1,4,8,8,1024]{4,3,2,1,0:T(8,128)(2,1)S(1)} %copy.130) | copy-start | bytes 1572868
  104.6 2.6 %copy-start.27 = (f32[1024]{0:T(1024)S(1)}, f32[1024]{0:T(1024)}, u32[]{:S(2)}) copy-start(f32[1024]{0:T(1024)} %param.13) | copy-start | bytes 12292
  107.5 13.1 %copy-start.9 = (bf16[256,1024]{1,0:T(8,128)(2,1)}, bf16[256,1024]{1,0:T(8,128)(2,1)S(1)}, u32[]{:S(2)}) copy-start(bf16[256,1024]{1,0:T(8,128)(2,1)S(1)} %get-tuple-element.50) | copy-start | bytes 1572868
  107.5 13.1 %copy-start.21 = (f32[256]{0:T(256)}, f32[256]{0:T(256)S(1)}, u32[]{:S(2)}) copy-start(f32[256]{0:T(256)S(1)} %broadcast_multiply_fusion.2) | copy-start | bytes 3076
  107.8 12.8 %copy-start.25 = (f32[256]{0:T(256)}, f32[256]{0:T(256)S(1)}, u32[]{:S(2)}) copy-start(f32[256]{0:T(256)S(1)} %add_rsqrt_fusion) | copy-start | bytes 3076
  112.4 8.1 %copy-start.23 = (f32[1024]{0:T(1024)S(1)}, f32[1024]{0:T(1024)}, u32[]{:S(2)}) copy-start(f32[1024]{0:T(1024)} %param.14) | copy-start | bytes 12292
  127.6 1.7 copy-start.11
  129.8 2.4 %copy-start.6 = (f32[4,12,64,64]{2,3,1,0:T(8,128)}, f32[4,12,64,64]{2,3,1,0:T(8,128)S(1)}, u32[]{:S(2)}) copy-start(f32[4,12,64,64]{2,3,1,0:T(8,128)S(1)} %add_select_fusion) | copy-start | bytes 2359300
  132.2 7.9 %copy-start.5 = (f32[4,12,64,64]{2,3,1,0:T(8,128)}, f32[4,12,64,64]{2,3,1,0:T(8,128)S(1)}, u32[]{:S(2)}) copy-start(f32[4,12,64,64]{2,3,1,0:T(8,128)S(1)} %get-tuple-element.52) | copy-start | bytes 2359300
  149.6 1.3 copy-start.13
  150.9 1.1 copy-start.12
  152.0 1.2 copy-start.10
  152.0 1.2 copy-start.18
  152.0 1.3 copy-start.19
  152.1 1.3 copy-start.22
  152.1 1.3 copy-start.24
  152.1 1.2 copy-start.26
  157.4 1.0 copy-start.8
  157.4 1.2 copy-start.20
  158.6 1.0 copy-start.17
  158.9 1.0 copy-start.16
  158.9 1.2 copy-start.15
  159.0 1.4 copy-start.14

commit v2 on v1

--- a/solution.py
+++ b/solution.py
@@ -501,6 +501,122 @@
     )(grad_blocks, small_blocks)
 
 
+def block_kernel(
+    heads, patch_ref, cot_ref, embed_ref, ebias_ref, gain_ref, qkv_ref, out_ref, bias_ref,
+    tag_col_ref, tag_row_ref,
+    grad_ref, egrad_ref, bgrad_ref, ggrad_ref, table_ref,
+    xhat_ref, proj_ref, datt_ref, att_ref, dproj_ref,
+):
+    f32, low = jnp.float32, jnp.bfloat16
+    groups = qkv_ref.shape[0]
+    share, part = qkv_ref.shape[2], out_ref.shape[2]
+    inner = out_ref.shape[1]
+    size = inner // heads
+    cells, features = cot_ref.shape
+    repeat = cells // bias_ref.shape[1]
+    scale = size ** (-0.5)
+    nt = (((1,), (1,)), ((), ()))
+    tn = (((0,), (0,)), ((), ()))
+
+    def dot(a, b, dims=(((1,), (0,)), ((), ()))):
+        return lax.dot_general(a, b, dims, preferred_element_type=f32)
+
+    gain = gain_ref[...]
+    rows = (dot(patch_ref[...], embed_ref[...]) + ebias_ref[...]).astype(low).astype(f32)
+    centered = rows - jnp.mean(rows, axis=1, keepdims=True)
+    inv_std = lax.rsqrt(jnp.mean(centered * centered, axis=1, keepdims=True) + norm_epsilon)
+    xhat_ref[...] = centered * inv_std
+    normed = (xhat_ref[...] * gain).astype(low)
+    total = None
+    for k in range(groups):
+        proj_ref[:, k * share : (k + 1) * share] = dot(normed, qkv_ref[k]).astype(low)
+        term = dot(cot_ref[:, k * part : (k + 1) * part], out_ref[k], nt)
+        total = term if total is None else total + term
+    datt_ref[...] = total.astype(low)
+    allowed = tag_col_ref[...] == tag_row_ref[...]
+    for h in range(heads):
+        q = proj_ref[:, h * size : (h + 1) * size]
+        key = proj_ref[:, inner + h * size : inner + (h + 1) * size]
+        v = proj_ref[:, 2 * inner + h * size : 2 * inner + (h + 1) * size]
+        da = datt_ref[:, h * size : (h + 1) * size]
+        bias = jnp.concatenate([bias_ref[h]] * repeat, axis=0)
+        scores = jnp.where(allowed, dot(q, key, nt) * scale + bias, -1e30)
+        weights = jnp.exp(scores - jnp.max(scores, axis=1, keepdims=True))
+        prob = weights / jnp.sum(weights, axis=1, keepdims=True)
+        prob_low = prob.astype(low)
+        att_ref[:, h * size : (h + 1) * size] = dot(prob_low, v).astype(low)
+        d_prob = dot(da, v, nt)
+        d_scores = prob * (d_prob - jnp.sum(prob * d_prob, axis=1, keepdims=True))
+        folded = d_scores[: cells // repeat]
+        for w in range(1, repeat):
+            folded = folded + d_scores[w * (cells // repeat) : (w + 1) * (cells // repeat)]
+        table_ref[h] = folded
+        d_low = d_scores.astype(low)
+        dproj_ref[:, h * size : (h + 1) * size] = (dot(d_low, key) * scale).astype(low)
+        dproj_ref[:, inner + h * size : inner + (h + 1) * size] = (
+            dot(d_low, q, tn) * scale
+        ).astype(low)
+        dproj_ref[:, 2 * inner + h * size : 2 * inner + (h + 1) * size] = dot(
+            prob_low, da, tn
+        ).astype(low)
+    d_normed = None
+    for k in range(groups):
+        grad_ref[k] = dot(att_ref[...], cot_ref[:, k * part : (k + 1) * part], tn).astype(low)
+        term = dot(dproj_ref[:, k * share : (k + 1) * share], qkv_ref[k], nt)
+        d_normed = term if d_normed is None else d_normed + term
+    xhat = xhat_ref[...]
+    ggrad_ref[...] = jnp.sum(d_normed * xhat, axis=0, keepdims=True)
+    g = d_normed * gain
+    branch = inv_std * (
+        g
+        - jnp.mean(g, axis=1, keepdims=True)
+        - xhat * jnp.mean(g * xhat, axis=1, keepdims=True)
+    )
+    branch = branch.astype(low)
+    patches = patch_ref[...]
+    egrad_ref[...] = dot(patches, cot_ref[...], tn) + dot(patches, branch, tn)
+    bgrad_ref[...] = jnp.sum(
+        cot_ref[...].astype(f32) + branch.astype(f32), axis=0, keepdims=True
+    )
+
+
+def block_grads(patch_rows, cot_rows, embed_weight, embed_bias, gain, qkv_all, out_all, bias_full, labels):
+    f32, low = jnp.float32, jnp.bfloat16
+    cells, features = cot_rows.shape
+    heads, span = bias_full.shape[:2]
+    inner = out_all.shape[1]
+    windows = cells // span
+    tags = (labels + 4 * jnp.arange(windows, dtype=jnp.int32)[:, None]).reshape(-1)
+    vmem = pl.BlockSpec(memory_space=VMEM)
+    shapes = [
+        (out_all.shape, low),
+        ((patch_rows.shape[1], features), f32),
+        ((1, features), f32),
+        ((1, features), f32),
+        ((heads, span, cells), f32),
+    ]
+    grad, egrad, bgrad, ggrad, table = pl.pallas_call(
+        functools.partial(block_kernel, heads),
+        out_shape=[jax.ShapeDtypeStruct(shape, kind) for shape, kind in shapes],
+        in_specs=[vmem] * 10,
+        out_specs=[vmem] * 5,
+        scratch_shapes=[
+            VMEM((cells, features), f32),
+            VMEM((cells, 3 * inner), low),
+            VMEM((cells, inner), low),
+            VMEM((cells, inner), low),
+            VMEM((cells, 3 * inner), low),
+        ],
+        compiler_params=pltpu.CompilerParams(vmem_limit_bytes=48 * 2**20),
+        name="block_grads",
+    )(
+        patch_rows, cot_rows, embed_weight, embed_bias[None], gain[None], qkv_all, out_all,
+        jnp.concatenate([bias_full] * windows, axis=2), tags[:, None], tags[None],
+    )
+    table_part = table.reshape(heads, span, windows, span).sum(axis=2)
+    return grad, egrad, bgrad[0], ggrad[0], table_part
+
+
 def on_device(
     direct,
     sizes,
@@ -524,12 +640,8 @@
         qkv_all, out_all, cot_r, cot_c, cot_x, pix_r, pix_c, pix_x = gather_inputs(
             sizes, qkv_weight, out_weight, cot_block, pix_block
         )
-        qkv_full = jnp.concatenate(
-            [w.reshape(-1, qkv_weight.shape[1]) for w in qkv_all], axis=1
-        )
-        out_full = jnp.concatenate(
-            [w.reshape(-1, out_weight.shape[1]) for w in out_all], axis=1
-        )
+        qkv_all = qkv_all.reshape(cols * dps, -1, qkv_weight.shape[1])
+        out_all = out_all.reshape(cols * dps, -1, out_weight.shape[1])
     else:
         qkv_full, out_full = [
             lax.all_gather(
@@ -576,29 +688,30 @@
     bias_full = jnp.dot(selector, bias_table.T, precision=lax.Precision.HIGHEST).T.reshape(
         head_count, WIN * WIN, WIN * WIN
     )
-    cells = embed_cells(patch_rows, embed_weight, embed_bias)
-    stored_residuals, attended = attend_forward(
-        cells.reshape(-1, WIN * WIN, features), labels, layer_norm_gain, qkv_full, bias_full
-    )
-    d_attended = lax.dot_general(
-        cot_flat, out_full, (((1,), (1,)), ((), ())), preferred_element_type=jnp.float32
-    ).astype(jnp.bfloat16)
-    d_rows, gain_contribution, table_part = attend_backward(
-        stored_residuals, d_attended, layer_norm_gain, qkv_full
-    )
-    table_grad = jnp.dot(
-        table_part.reshape(head_count, -1), selector, precision=lax.Precision.HIGHEST
-    )
     contract = (((0,), (0,)), ((), ()))
-    back_rows = jnp.concatenate([cot_flat, d_rows], axis=0)
-    embed_grad = lax.dot_general(
-        jnp.concatenate([patch_rows, patch_rows], axis=0),
-        back_rows,
-        contract,
-        preferred_element_type=jnp.float32,
-    )
-    bias_grad = jnp.sum(back_rows, axis=0, dtype=jnp.float32)
     if not direct:
+        cells = embed_cells(patch_rows, embed_weight, embed_bias)
+        stored_residuals, attended = attend_forward(
+            cells.reshape(-1, WIN * WIN, features), labels, layer_norm_gain, qkv_full, bias_full
+        )
+        d_attended = lax.dot_general(
+            cot_flat, out_full, (((1,), (1,)), ((), ())), preferred_element_type=jnp.float32
+        ).astype(jnp.bfloat16)
+        d_rows, gain_contribution, table_part = attend_backward(
+            stored_residuals, d_attended, layer_norm_gain, qkv_full
+        )
+        table_grad = jnp.dot(
+            table_part.reshape(head_count, -1), selector, precision=lax.Precision.HIGHEST
+        )
+        contract = (((0,), (0,)), ((), ()))
+        back_rows = jnp.concatenate([cot_flat, d_rows], axis=0)
+        embed_grad = lax.dot_general(
+            jnp.concatenate([patch_rows, patch_rows], axis=0),
+            back_rows,
+            contract,
+            preferred_element_type=jnp.float32,
+        )
+        bias_grad = jnp.sum(back_rows, axis=0, dtype=jnp.float32)
         partial_rows = lax.psum_scatter(
             lax.dot_general(attended, cot_flat, contract, preferred_element_type=jnp.float32),
             "row",
@@ -613,15 +726,14 @@
         )
         return (out_weight_grad,) + totals
     groups = cols * dps
-    cot_groups = cot_flat.reshape(-1, groups, features // groups)
-    grad_blocks = jnp.stack(
-        [
-            lax.dot_general(
-                attended, cot_groups[:, k], contract, preferred_element_type=jnp.float32
-            ).astype(jnp.bfloat16)
-            for k in range(groups)
-        ]
-    ).reshape((groups, rows) + out_weight.shape)
+    grad_blocks, embed_grad, bias_grad, gain_contribution, table_part = block_grads(
+        patch_rows, cot_flat, embed_weight, embed_bias, layer_norm_gain, qkv_all, out_all,
+        bias_full, labels,
+    )
+    grad_blocks = grad_blocks.reshape((groups, rows) + out_weight.shape)
+    table_grad = jnp.dot(
+        table_part.reshape(head_count, -1), selector, precision=lax.Precision.HIGHEST
+    )
     pieces = (embed_grad, bias_grad, gain_contribution, table_grad)
     flat = jnp.concatenate([piece.reshape(-1) for piece in pieces])
     unit = groups * rows * 2048

time: 204 us -> 168 us (0.82)
  local copies, waits for them, and re-layouts: 43.5 us -> 19.4 us
  matrix products: 25.7 us -> 4 us
  Pallas kernels: 121 us -> 136 us
  other arithmetic: 6.65 us -> 2.58 us
    dot_general x15 -> x0, matrix products: 21.5 us -> none  [the longest x1 4.13 us: attend_backward(): jnp.einsum('whmn,wmhd->wnhd', reduced_probability, d_heads, preferred_ele...]
    pallas_call x0 -> x1, Pallas kernels: none -> 15.1 us  [block_grads(): pl.pallas_call(functools.partial(block_kernel, heads), out_shape=[jax.Sha...]
    reshape x11 -> x2, local copies, waits for them, and re-layouts: 10.4 us -> 2.29 us  [the longest x1 2.12 us: block_grads(): table_part = table.reshape(heads, span, windows, span).sum(axis=2)]
    concatenate x1 -> x0, local copies, waits for them, and re-layouts: 8.12 us -> none  [on_device(): jnp.concatenate([w.reshape(-1, qkv_weight.shape[1]) for w in qkv_all], ax...]
    another operation x4 -> x2, local copies, waits for them, and re-layouts: 5.84 us -> 0.18 us  [on_device(): labels = window_split(region[:, :, None])[:, :, 0]]
    convert_element_type x4 -> x0, local copies, waits for them, and re-layouts: 2.68 us -> none  [the longest x1 0.85 us: attend_backward(): d_keys = (jnp.einsum('whmn,wmhd->wnhd', d_low, query_rows, preferred_elem...]
    sub x1 -> x0, other arithmetic: 2.35 us -> none  [attend_forward(): exp_scores = jnp.exp(scores - row_peak)]
    convert_element_type x2 -> x0, other arithmetic: 2.31 us -> none  [the longest x1 1.94 us: attend_backward(): d_low = d_scores.astype(jnp.bfloat16)]
where the time goes in v2:
time: 168 us
  Pallas kernels  136 us (81%)
  local copies, waits for them, and re-layouts  19.4 us (12%)
  between operations  6.12 us (4%)
  matrix products  4 us (2%)
  other arithmetic  2.58 us (2%)
    pallas_call x1, Pallas kernels, gather_inputs(): pl.pallas_call(functools.partial(gather_kernel, sizes), out_shape=[jax.Sh...  81.5 us
    pallas_call x1, Pallas kernels, reduce_outputs(): pl.pallas_call(functools.partial(reduce_kernel, sizes), out_shape=[jax.Sh...  39.4 us
    pallas_call x1, Pallas kernels, block_grads(): pl.pallas_call(functools.partial(block_kernel, heads), out_shape=[jax.Sha...  15.1 us
    unnamed x26, local copies, waits for them, and re-layouts  6.29 us

profile of v2, /device:TPU:0, one launch (start us, length us, event | category | flops | bytes accessed | tf_op | source)
XLA Modules:
  0.0 168.0 jit_solution(13075587776835002301)
XLA Ops:
  0.6 0.0 copy-start
  0.7 1.3 fusion.9
  7.2 0.1 add.90
  7.3 0.1 add.93
  7.3 0.1 add.91
  7.4 0.1 add_bitcast_fusion
  7.5 0.1 squeeze_reshape.10
  7.6 0.1 squeeze_reshape.9
  7.7 0.8 eq.15
  8.5 0.1 copy.28.tag_col_ref
  8.7 0.0 copy-start.2
  8.7 0.0 copy-start.7
  8.7 0.0 copy-start.8
  8.7 1.1 copy.23.qkv_ref
  9.8 0.0 copy-done
  9.8 2.6 %convolution_bitcast_fusion = f32[12,4096]{1,0:T(8,128)S(1)} fusion(f32[12,225]{1,0:T(8,128)S(1)} %copy-done, s32[4096]{0:T(1024)S(1)} %eq.15), kind=kOutput, calls=%fused_computation | convolution fusion | flops 133632000 | bytes 223792 | tf_op jit(solution)/shard_map/dot_general | solution.py:688
  12.4 0.2 reshape.133
  12.6 0.4 pad_maximum_fusion.bias_ref
  13.0 0.0 copy-done.2
  13.0 0.0 copy-done.7
  13.0 0.0 copy-done.8
  13.0 81.5 %gather_inputs.1 = (bf16[4,8,128,576]{3,2,1,0:T(8,128)(2,1)S(1)}, bf16[4,8,96,256]{3,2,1,0:T(8,128)(2,1)S(1)}, bf16[8,32,1024]{2,1,0:T(8,128)(2,1)S(1)}, bf16[8,...) custom-call(bf16[128,576]{1,0:T(8,128)(2,1)S(1)} %copy.23.qkv_ref, ...), custom_call_target="tpu_custom_call" | custom-call | tf_op jit(solution)/shard_map/gather_inputs/pallas_call | solution.py:321
  94.5 0.0 copy-start.1
  94.5 2.3 %copy-done.1 = bf16[4,8,128,576]{3,2,1,0:T(8,128)(2,1)} copy-done((bf16[4,8,128,576]{3,2,1,0:T(8,128)(2,1)}, bf16[4,8,128,576]{3,2,1,0:T(8,128)(2,1)S(1)}, u32[]{:S(2)}) %copy-start.1) | copy-done | bytes 4718616
  96.8 1.1 fusion.5
  98.0 2.6 %reshape_broadcast_in_dim.4 = bf16[1,3,16,4,40,4]{5,4,3,2,1,0:T(8,128)(2,1)} reshape(bf16[3,64,160]{2,1,0:T(8,128)(2,1)S(1)} %maximum_maximum_fusion) | data formatting | bytes 122880 | tf_op jit(solution)/shard_map/reshape;broadcast_in_dim | solution.py:27
  100.6 0.0 copy-start.6
  100.6 0.0 copy-start.9
  100.6 0.0 copy-start.10
  100.6 2.8 %copy.24 = bf16[1,16,40,3,4,4]{2,1,5,4,3,0:T(8,128)(2,1)S(1)} copy(bf16[1,16,40,3,4,4]{5,2,4,1,3,0:T(8,128)(2,1)} %bitcast.61) | data formatting | bytes 122880 | tf_op jit(solution)/shard_map/transpose | solution.py:28
  103.4 0.1 constant_dynamic-slice_fusion
  103.5 0.1 copy.25
  103.7 0.0 copy-done.6
  103.7 0.0 copy-done.9
  103.7 0.0 copy-done.10
  103.7 15.1 %block_grads.1 = (bf16[4,768,256]{2,1,0:T(8,128)(2,1)S(1)}, f32[48,1024]{1,0:T(8,128)S(1)}, f32[1,1024]{1,0:T(1,128)S(1)}, f32[1,1024]{1,0:T(1,128)S(1)}, f32[12,64,256]{2,1,0:T(8,128)S(1)}) custom-call(bf16[256,48]{1,0:T(8,128)(2,1)S(1)} %bitcast.51, bf16[256,1024]{1,0:T(8,128)(2,1)S(1)} %bitcast.47, bf16[48,1024]{1,0:T(8,128)(2,1)S(1)} %copy-done.6, ...), custom_call_target="tpu_custom_call" | custom-call | tf_op jit(solution)/shard_map/block_grads/pallas_call | solution.py:598
  118.8 0.0 copy-start.3
  118.8 1.2 copy-done.3
  119.9 0.0 copy-start.5
  119.9 0.9 copy-done.5
  120.9 2.1 %reshape.136 = f32[12,64,4,64]{3,2,1,0:T(4,128)S(1)} reshape(f32[12,64,256]{2,1,0:T(8,128)} %copy-done.5) | data formatting | bytes 1572864 | tf_op jit(solution)/shard_map/reshape | solution.py:616
  123.0 1.0 reduce_sum.9
  124.0 0.0 copy-start.4
  124.0 0.1 reshape.137
  124.1 1.4 fusion
  125.5 0.1 reshape.138
  125.7 0.1 reshape.139.small_ref
  125.8 0.0 copy-done.4
  125.8 39.4 %reduce_outputs.1 = (f32[96,256]{1,0:T(8,128)S(1)}, f32[4,8,8,256]{3,2,1,0:T(8,128)S(1)}) custom-call(bf16[4,8,96,256]{3,2,1,0:T(8,128)(2,1)S(1)} %bitcast.49, f32[4,8,8,256]{3,2,1,0:T(8,128)S(1)} %reshape.139.small_ref), custom_call_target="tpu_custom_call" | custom-call | tf_op jit(solution)/shard_map/reduce_outputs/pallas_call | solution.py:477
  165.2 0.7 reshape.140
  165.9 0.1 copy.30
  166.0 0.6 fusion.8
  166.6 0.7 reshape.142
  167.3 0.6 copy.32
  (12 shorter events, 0.2 us)
Async XLA Ops:
  0.6 9.2 %copy-start = (f32[12,225]{1,0:T(8,128)S(1)}, f32[12,225]{1,0:T(8,128)}, u32[]{:S(2)}) copy-start(f32[12,225]{1,0:T(8,128)} %param.17) | copy-start | bytes 32404
  8.7 4.3 %copy-start.2 = (bf16[1,8,32,1024]{3,2,1,0:T(8,128)(2,1)S(1)}, bf16[1,8,32,1024]{3,2,1,0:T(8,128)(2,1)}, u32[]{:S(2)}) copy-start(bf16[1,8,32,1024]{3,2,1,0:T(8,128)(2,1)} %param.11) | copy-start | bytes 1572868
  8.7 4.3 %copy-start.7 = (bf16[1,3,32,128]{3,2,1,0:T(8,128)(2,1)S(1)}, bf16[1,3,32,128]{3,2,1,0:T(8,128)(2,1)}, u32[]{:S(2)}) copy-start(bf16[1,3,32,128]{3,2,1,0:T(8,128)(2,1)} %param.10) | copy-start | bytes 73732
  8.7 4.3 %copy-start.8 = (bf16[96,256]{1,0:T(8,128)(2,1)S(1)}, bf16[96,256]{1,0:T(8,128)(2,1)}, u32[]{:S(2)}) copy-start(bf16[96,256]{1,0:T(8,128)(2,1)} %out_ref.1) | copy-start | bytes 147460
  94.5 2.3 %copy-start.1 = (bf16[4,8,128,576]{3,2,1,0:T(8,128)(2,1)}, bf16[4,8,128,576]{3,2,1,0:T(8,128)(2,1)S(1)}, u32[]{:S(2)}) copy-start(bf16[4,8,128,576]{3,2,1,0:T(8,128)(2,1)S(1)} %get-tuple-element.26) | copy-start | bytes 14155780
  100.6 3.1 %copy-start.6 = (bf16[48,1024]{1,0:T(8,128)(2,1)S(1)}, bf16[48,1024]{1,0:T(8,128)(2,1)}, u32[]{:S(2)}) copy-start(bf16[48,1024]{1,0:T(8,128)(2,1)} %embed_ref.1) | copy-start | bytes 294916
  100.6 3.1 %copy-start.9 = (f32[1024]{0:T(1024)S(1)}, f32[1024]{0:T(1024)}, u32[]{:S(2)}) copy-start(f32[1024]{0:T(1024)} %param.13) | copy-start | bytes 12292
  100.6 3.1 %copy-start.10 = (f32[1024]{0:T(1024)S(1)}, f32[1024]{0:T(1024)}, u32[]{:S(2)}) copy-start(f32[1024]{0:T(1024)} %param.14) | copy-start | bytes 12292
  118.8 1.2 copy-start.3
  119.9 0.9 copy-start.5
  124.0 1.8 %copy-start.4 = (bf16[4,768,256]{2,1,0:T(8,128)(2,1)S(1)}, bf16[4,768,256]{2,1,0:T(8,128)(2,1)}, u32[]{:S(2)}) copy-start(bf16[4,768,256]{2,1,0:T(8,128)(2,1)} %copy-done.3) | copy-start | bytes 4718596

commit v3 on v2

--- a/solution.py
+++ b/solution.py
@@ -224,25 +224,12 @@
 
     over_y = {"dp": (dp + 1) % 2}
     over_x = {"row": z * 2 + (x + 1) % 2}
-    up = {"row": ((z + 1) % ring) * 2 + x}
-    down = {"row": ((z + ring - 1) % ring) * 2 + x}
     over_core = {"col": (col + 1) % 2}
-
-    def onward_up(dy, dx, dz):
-        if dz + 1 < ring // 2 or (dz + 1 == ring // 2 and dy == 0):
-            send((0, dy, dx, dz), up, (0, dy, dx, dz + 1))
-
-    def onward_down(dy, dx, back):
-        if back + 1 < ring // 2 or (back + 1 == ring // 2 and dy == 1):
-            send((0, dy, dx, (ring - back) % ring), down, (0, dy, dx, ring - back - 1))
-
-    def spread(dy, dx):
-        onward_up(dy, dx, 0)
-        onward_down(dy, dx, 0)
-
+    along = [s for s in range(1, ring) if s != ring // 2] + [ring // 2]
+    for s in along:
+        send((0, 0, 0, 0), {"row": ((z + s) % ring) * 2 + x}, (0, 0, 0, s))
     send((0, 0, 0, 0), over_y, (0, 1, 0, 0))
     send((0, 0, 0, 0), over_x, (0, 0, 1, 0))
-    spread(0, 0)
     send((0, 0, 0, 0), over_core, (1, 0, 0, 0))
     local = [
         pltpu.make_async_copy(own[array], slot(array, (0, 0, 0, 0)), own_sem.at[array])
@@ -250,9 +237,14 @@
     ]
     for copy in local:
         copy.start()
-    arrive((0, 1, 0, 0))
-    send((0, 1, 0, 0), over_x, (0, 1, 1, 0))
-    spread(1, 0)
+    arrive((0, 0, 1, 0))
+    send((0, 0, 1, 0), over_y, (0, 1, 1, 0))
+    send((0, 0, 1, 0), over_core, (1, 0, 1, 0))
+    for s in along:
+        arrive((0, 0, 0, s))
+        send((0, 0, 0, s), over_x, (0, 0, 1, s))
+        send((0, 0, 0, s), over_y, (0, 1, 0, s))
+        send((0, 0, 0, s), over_core, (1, 0, 0, s))
     above = (row + rows - 1) % rows
     left = (col + cols - 1) % cols
     edge = cot_c.shape[1]
@@ -275,22 +267,13 @@
         )
         copy.start()
         halos.append(copy)
-    send((0, 1, 0, 0), over_core, (1, 1, 0, 0))
-    for dy in range(2):
-        arrive((0, dy, 1, 0))
-        spread(dy, 1)
-        send((0, dy, 1, 0), over_core, (1, dy, 1, 0))
-    for step in range(1, ring // 2 + 1):
-        for dx in range(2):
-            for dy in range(2):
-                if step < ring // 2 or dy == 0:
-                    arrive((0, dy, dx, step))
-                    onward_up(dy, dx, step)
-                    send((0, dy, dx, step), over_core, (1, dy, dx, step))
-                if step < ring // 2 or dy == 1:
-                    arrive((0, dy, dx, ring - step))
-                    onward_down(dy, dx, step)
-                    send((0, dy, dx, ring - step), over_core, (1, dy, dx, ring - step))
+    for s in along:
+        arrive((0, 0, 1, s))
+        send((0, 0, 1, s), over_y, (0, 1, 1, s))
+        send((0, 0, 1, s), over_core, (1, 0, 1, s))
+    for dx, dz in [(0, 0), (1, 0)] + [(0, s) for s in along] + [(1, s) for s in along]:
+        arrive((0, 1, dx, dz))
+        send((0, 1, dx, dz), over_core, (1, 1, dx, dz))
     for dz in range(ring):
         for dx in range(2):
             for dy in range(2):

time: 168 us -> 143 us (0.85)
  Pallas kernels: 136 us -> 110 us
    pallas_call x1, Pallas kernels: 81.5 us -> 49.6 us  [gather_inputs(): pl.pallas_call(functools.partial(gather_kernel, sizes), out_shape=[jax.Sh...]
    pallas_call x1, Pallas kernels: 39.4 us -> 45.4 us  [reduce_outputs(): pl.pallas_call(functools.partial(reduce_kernel, sizes), out_shape=[jax.Sh...]
where the time goes in v3:
time: 143 us; the launch traced here: 142 us
  Pallas kernels  110 us (77%)
  local copies, waits for them, and re-layouts  19.4 us (14%)
  between operations  6.12 us (4%)
  matrix products  4 us (3%)
  other arithmetic  2.59 us (2%)
    pallas_call x1, Pallas kernels, gather_inputs(): pl.pallas_call(functools.partial(gather_kernel, sizes), out_shape=[jax.Sh...  49.6 us
    pallas_call x1, Pallas kernels, reduce_outputs(): pl.pallas_call(functools.partial(reduce_kernel, sizes), out_shape=[jax.Sh...  45.4 us
    pallas_call x1, Pallas kernels, block_grads(): pl.pallas_call(functools.partial(block_kernel, heads), out_shape=[jax.Sha...  15.1 us
    unnamed x26, local copies, waits for them, and re-layouts  6.29 us

profile of v3, /device:TPU:0, one launch (start us, length us, event | category | flops | bytes accessed | tf_op | source)
XLA Modules:
  0.0 142.1 jit_solution(12250484630408215290)
XLA Ops:
  0.6 0.0 copy-start
  0.7 1.3 fusion.9
  7.2 0.1 add.90
  7.3 0.1 add.93
  7.3 0.1 add.91
  7.4 0.1 add_bitcast_fusion
  7.5 0.1 squeeze_reshape.10
  7.6 0.1 squeeze_reshape.9
  7.7 0.8 eq.15
  8.5 0.1 copy.28.tag_col_ref
  8.7 0.0 copy-start.2
  8.7 0.0 copy-start.7
  8.7 0.0 copy-start.8
  8.7 1.1 copy.23.qkv_ref
  9.8 0.0 copy-done
  9.8 2.6 %convolution_bitcast_fusion = f32[12,4096]{1,0:T(8,128)S(1)} fusion(f32[12,225]{1,0:T(8,128)S(1)} %copy-done, s32[4096]{0:T(1024)S(1)} %eq.15), kind=kOutput, calls=%fused_computation | convolution fusion | flops 133632000 | bytes 223792 | tf_op jit(solution)/shard_map/dot_general | solution.py:671
  12.4 0.2 reshape.133
  12.6 0.4 pad_maximum_fusion.bias_ref
  13.0 0.0 copy-done.2
  13.0 0.0 copy-done.7
  13.0 0.0 copy-done.8
  13.0 49.6 %gather_inputs.1 = (bf16[4,8,128,576]{3,2,1,0:T(8,128)(2,1)S(1)}, bf16[4,8,96,256]{3,2,1,0:T(8,128)(2,1)S(1)}, bf16[8,32,1024]{2,1,0:T(8,128)(2,1)S(1)}, bf16[8,...) custom-call(bf16[128,576]{1,0:T(8,128)(2,1)S(1)} %copy.23.qkv_ref, ...), custom_call_target="tpu_custom_call" | custom-call | tf_op jit(solution)/shard_map/gather_inputs/pallas_call | solution.py:304
  62.6 0.0 copy-start.1
  62.6 2.3 %copy-done.1 = bf16[4,8,128,576]{3,2,1,0:T(8,128)(2,1)} copy-done((bf16[4,8,128,576]{3,2,1,0:T(8,128)(2,1)}, bf16[4,8,128,576]{3,2,1,0:T(8,128)(2,1)S(1)}, u32[]{:S(2)}) %copy-start.1) | copy-done | bytes 4718616
  64.9 1.1 fusion.5
  66.1 2.6 %reshape_broadcast_in_dim.4 = bf16[1,3,16,4,40,4]{5,4,3,2,1,0:T(8,128)(2,1)} reshape(bf16[3,64,160]{2,1,0:T(8,128)(2,1)S(1)} %maximum_maximum_fusion) | data formatting | bytes 122880 | tf_op jit(solution)/shard_map/reshape;broadcast_in_dim | solution.py:27
  68.7 0.0 copy-start.6
  68.7 0.0 copy-start.9
  68.7 0.0 copy-start.10
  68.7 2.8 %copy.24 = bf16[1,16,40,3,4,4]{2,1,5,4,3,0:T(8,128)(2,1)S(1)} copy(bf16[1,16,40,3,4,4]{5,2,4,1,3,0:T(8,128)(2,1)} %bitcast.61) | data formatting | bytes 122880 | tf_op jit(solution)/shard_map/transpose | solution.py:28
  71.5 0.1 constant_dynamic-slice_fusion
  71.7 0.1 copy.25
  71.8 0.0 copy-done.6
  71.8 0.0 copy-done.9
  71.8 0.0 copy-done.10
  71.8 15.1 %block_grads.1 = (bf16[4,768,256]{2,1,0:T(8,128)(2,1)S(1)}, f32[48,1024]{1,0:T(8,128)S(1)}, f32[1,1024]{1,0:T(1,128)S(1)}, f32[1,1024]{1,0:T(1,128)S(1)}, f32[12,64,256]{2,1,0:T(8,128)S(1)}) custom-call(bf16[256,48]{1,0:T(8,128)(2,1)S(1)} %bitcast.51, bf16[256,1024]{1,0:T(8,128)(2,1)S(1)} %bitcast.47, bf16[48,1024]{1,0:T(8,128)(2,1)S(1)} %copy-done.6, ...), custom_call_target="tpu_custom_call" | custom-call | tf_op jit(solution)/shard_map/block_grads/pallas_call | solution.py:581
  86.9 0.0 copy-start.3
  86.9 1.2 copy-done.3
  88.1 0.0 copy-start.5
  88.1 0.9 copy-done.5
  89.0 2.1 %reshape.136 = f32[12,64,4,64]{3,2,1,0:T(4,128)S(1)} reshape(f32[12,64,256]{2,1,0:T(8,128)} %copy-done.5) | data formatting | bytes 1572864 | tf_op jit(solution)/shard_map/reshape | solution.py:599
  91.1 1.0 reduce_sum.9
  92.1 0.0 copy-start.4
  92.1 0.1 reshape.137
  92.2 1.4 %fusion = f32[12,225]{1,0:T(8,128)S(1)} fusion(f32[12,4096]{1,0:T(8,128)S(1)} %reshape.137, s32[4096]{0:T(1024)S(1)} %eq.15), kind=kOutput, calls=%fused_computation.2 | convolution fusion | flops 133632000 | bytes 223792 | tf_op jit(solution)/shard_map/dot_general | solution.py:717
  93.7 0.1 reshape.138
  93.8 0.1 reshape.139.small_ref
  93.9 0.0 copy-done.4
  93.9 45.4 %reduce_outputs.1 = (f32[96,256]{1,0:T(8,128)S(1)}, f32[4,8,8,256]{3,2,1,0:T(8,128)S(1)}) custom-call(bf16[4,8,96,256]{3,2,1,0:T(8,128)(2,1)S(1)} %bitcast.49, f32[4,8,8,256]{3,2,1,0:T(8,128)S(1)} %reshape.139.small_ref), custom_call_target="tpu_custom_call" | custom-call | tf_op jit(solution)/shard_map/reduce_outputs/pallas_call | solution.py:460
  139.3 0.7 reshape.140
  140.0 0.1 copy.30
  140.2 0.6 fusion.8
  140.8 0.7 reshape.142
  141.5 0.6 copy.32
  (12 shorter events, 0.2 us)
Async XLA Ops:
  0.6 9.2 %copy-start = (f32[12,225]{1,0:T(8,128)S(1)}, f32[12,225]{1,0:T(8,128)}, u32[]{:S(2)}) copy-start(f32[12,225]{1,0:T(8,128)} %param.17) | copy-start | bytes 32404
  8.7 4.3 %copy-start.2 = (bf16[1,8,32,1024]{3,2,1,0:T(8,128)(2,1)S(1)}, bf16[1,8,32,1024]{3,2,1,0:T(8,128)(2,1)}, u32[]{:S(2)}) copy-start(bf16[1,8,32,1024]{3,2,1,0:T(8,128)(2,1)} %param.11) | copy-start | bytes 1572868
  8.7 4.3 %copy-start.7 = (bf16[1,3,32,128]{3,2,1,0:T(8,128)(2,1)S(1)}, bf16[1,3,32,128]{3,2,1,0:T(8,128)(2,1)}, u32[]{:S(2)}) copy-start(bf16[1,3,32,128]{3,2,1,0:T(8,128)(2,1)} %param.10) | copy-start | bytes 73732
  8.7 4.3 %copy-start.8 = (bf16[96,256]{1,0:T(8,128)(2,1)S(1)}, bf16[96,256]{1,0:T(8,128)(2,1)}, u32[]{:S(2)}) copy-start(bf16[96,256]{1,0:T(8,128)(2,1)} %out_ref.1) | copy-start | bytes 147460
  62.6 2.3 %copy-start.1 = (bf16[4,8,128,576]{3,2,1,0:T(8,128)(2,1)}, bf16[4,8,128,576]{3,2,1,0:T(8,128)(2,1)S(1)}, u32[]{:S(2)}) copy-start(bf16[4,8,128,576]{3,2,1,0:T(8,128)(2,1)S(1)} %get-tuple-element.26) | copy-start | bytes 14155780
  68.7 3.1 %copy-start.6 = (bf16[48,1024]{1,0:T(8,128)(2,1)S(1)}, bf16[48,1024]{1,0:T(8,128)(2,1)}, u32[]{:S(2)}) copy-start(bf16[48,1024]{1,0:T(8,128)(2,1)} %embed_ref.1) | copy-start | bytes 294916
  68.7 3.1 %copy-start.9 = (f32[1024]{0:T(1024)S(1)}, f32[1024]{0:T(1024)}, u32[]{:S(2)}) copy-start(f32[1024]{0:T(1024)} %param.13) | copy-start | bytes 12292
  68.7 3.1 %copy-start.10 = (f32[1024]{0:T(1024)S(1)}, f32[1024]{0:T(1024)}, u32[]{:S(2)}) copy-start(f32[1024]{0:T(1024)} %param.14) | copy-start | bytes 12292
  86.9 1.2 copy-start.3
  88.1 0.9 copy-start.5
  92.1 1.8 %copy-start.4 = (bf16[4,768,256]{2,1,0:T(8,128)(2,1)S(1)}, bf16[4,768,256]{2,1,0:T(8,128)(2,1)}, u32[]{:S(2)}) copy-start(bf16[4,768,256]{2,1,0:T(8,128)(2,1)} %copy-done.3) | copy-start | bytes 4718596
